TPU v7x, 8 devices: a whole 2x2x1 slice. The times are simulated.
8 devices in a mesh: batch: 1 (over z), w: 2 (over y), h: 4 (over x, core).
Axes of the slice: x: 2, y: 2, z: 1, core: 2. Of those that a mesh axis runs over, the one named last changes fastest.
Arguments:
- image: bfloat16 [128, 64, 512, 3], P('batch', 'h', 'w')
- down_w1: bfloat16 [3, 3, 3, 64], replicated
- down_v1: float32 [3, 64], replicated
- refine_w1: bfloat16 [3, 3, 64, 64], replicated
- refine_v1: float32 [3, 64], replicated
- down_w2: bfloat16 [3, 3, 64, 128], replicated
- down_v2: float32 [3, 128], replicated
- refine_w2: bfloat16 [3, 3, 128, 128], replicated
- refine_v2: float32 [3, 128], replicated
- down_w3: bfloat16 [3, 3, 128, 256], replicated
- down_v3: float32 [3, 256], replicated
- refine_w3: bfloat16 [3, 3, 256, 256], replicated
- refine_v3: float32 [3, 256], replicated
Outputs:
- output: bfloat16 [128, 8, 64, 256], P('batch', 'h', 'w')
All inputs are finite; a program needn't handle non-finite values.
Results may differ from a plain program's by a relative error of at most 0.00400014.
Values are sent between devices in bfloat16 or wider.
A program may use at most 1 GiB of HBM per device.

v0:
```python
import jax
import jax.numpy as jnp
from jax import lax
from jax.sharding import PartitionSpec as P

NORM_GROUPS = 8
NORM_EPS = 1e-5


def shift_in(piece, axis_name, axis_size, from_lower):
    if axis_size == 1:
        return jnp.zeros_like(piece)
    if from_lower:
        send_pairs = [(source, source + 1) for source in range(axis_size - 1)]
    else:
        send_pairs = [(source + 1, source) for source in range(axis_size - 1)]
    return lax.ppermute(piece, axis_name, send_pairs)


def lower_halo(tile, row_count, col_count):
    above = shift_in(tile[:, -1:], "h", row_count, True)
    tall = jnp.concatenate([above, tile], axis=1)
    left = shift_in(tall[:, :, -1:], "w", col_count, True)
    return jnp.concatenate([left, tall], axis=2)


def both_halo(tile, row_count, col_count):
    above = shift_in(tile[:, -1:], "h", row_count, True)
    below = shift_in(tile[:, :1], "h", row_count, False)
    tall = jnp.concatenate([above, tile, below], axis=1)
    left = shift_in(tall[:, :, -1:], "w", col_count, True)
    right = shift_in(tall[:, :, :1], "w", col_count, False)
    return jnp.concatenate([left, tall, right], axis=2)


def norm_apply(summed, affine, totals, pixel_count, per_group):
    grp_mean = totals[0] / pixel_count
    grp_var = jnp.maximum(totals[1] / pixel_count - jnp.square(grp_mean), 0.0)
    inv_std = lax.rsqrt(grp_var + NORM_EPS)
    chan_scale = jnp.repeat(inv_std, per_group, axis=1) * affine[1]
    chan_shift = affine[2] - jnp.repeat(grp_mean * inv_std, per_group, axis=1) * affine[1]
    return jax.nn.relu(summed * chan_scale[:, None, None, :] + chan_shift[:, None, None, :]).astype(jnp.bfloat16)


def conv_norm(padded, kernel, affine, stride, spatial_devices):
    summed = lax.conv_general_dilated(padded, kernel, (stride, stride), "VALID", dimension_numbers=("NHWC", "HWIO", "NHWC"), preferred_element_type=jnp.float32) + affine[0]
    out_shape = summed.shape
    per_group = out_shape[3] // NORM_GROUPS
    pixel_count = out_shape[1] * out_shape[2] * spatial_devices * per_group
    part_sums = jnp.stack([jnp.sum(summed, axis=(1, 2)), jnp.sum(jnp.square(summed), axis=(1, 2))])
    part_sums = jnp.sum(part_sums.reshape(2, out_shape[0], NORM_GROUPS, per_group), axis=3)
    totals = lax.psum(part_sums, ("h", "w"))
    return norm_apply(summed, affine, totals, pixel_count, per_group)


def solution(mesh):
    row_count = mesh.shape["h"]
    col_count = mesh.shape["w"]
    spatial_devices = row_count * col_count
    act_spec = P("batch", "h", "w")

    def local_forward(tile, *params):
        current = tile
        for stage in range(3):
            down_w, down_v, refine_w, refine_v = params[4 * stage:4 * stage + 4]
            current = conv_norm(lower_halo(current, row_count, col_count), down_w, down_v, 2, spatial_devices)
            current = conv_norm(both_halo(current, row_count, col_count), refine_w, refine_v, 1, spatial_devices)
        return current

    return jax.shard_map(local_forward, mesh=mesh, in_specs=(act_spec,) + (P(),) * 12, out_specs=act_spec, check_vma=False)
```

profile of v0, /device:TPU:0, one launch (start us, length us, event | category | flops | bytes accessed | tf_op | source)
XLA Modules:
  0.0 522.6 jit_solution(15454485243596485224)
XLA Ops:
  0.0 6.2 %copy.36 = bf16[128,16,256,3]{0,3,2,1:T(4,128)(2,1)} copy(bf16[128,16,256,3]{2,1,3,0:T(8,128)(2,1)} %param.13) | data formatting | bytes 6291456 | tf_op args[0]
  7.2 2.8 collective-permute-start
  11.9 4.3 collective-permute-start.1
  17.6 16.8 %add_reduce_fusion.1 = (f32[128,64]{0,1:T(8,128)S(1)}, f32[128,64]{0,1:T(8,128)S(1)}, f32[128,8,128,64]{0,3,2,1:T(8,128)}) fusion(f32[64]{0:T(128)S(1)} %get-tuple-element.57, bf16[3,3,3,64]{3,2,1,0:T(4,128)(2,1)S(1)} %copy-done.14, bf16[128,16,256,3]{0,3,2,1:T(4,128)(2,1)} %copy.36, bf16[128,1,256,3]{0,3,2,1:T(4,128)(2,1)S(1)} %collective-permute-done, ...), kind=kOutput, calls=%fused_computation.5 | convolution fusion | flops 496589056 | bytes 36979072 | tf_op jit(solution)/shard_map/conv_general_dilated | solution.py:46
  34.4 28.9 %psum.42 = f32[2,128,8]{1,2,0:T(8,128)S(1)} all-reduce(f32[2,128,8]{1,2,0:T(8,128)S(1)} %maximum_reduce_fusion.4), channel_id=1, replica_groups=mesh['batch'=1,'w'=2,'h'=4] {'h','w'}, use_global_device_ids=true, to_apply=%region_3.0 | all-reduce | flops 2048 | bytes 16384 | tf_op jit(solution)/shard_map/psum | solution.py:52
  63.4 14.3 %maximum_convert_fusion.1 = bf16[128,8,128,64]{0,3,2,1:T(8,128)(2,1)S(1)} fusion(f32[128,8,128,64]{0,3,2,1:T(8,128)} %get-tuple-element.71, f32[128,64]{0,1:T(8,128)S(1)} %get-tuple-element.70, f32[128,64]{0,1:T(8,128)S(1)} %get-tuple-element.69, f32[64]{0:T(128)S(1)} %get-tuple-element.57), kind=kLoop, calls=%fused_computation.2 | loop fusion | flops 41943040 | bytes 50397440 | tf_op jit(solution)/shard_map/convert_element_type | solution.py:42
  78.7 1.4 collective-permute-start.2
  80.1 1.4 collective-permute-start.3
  81.6 2.2 collective-permute-done.2
  83.7 5.0 collective-permute-done.3
  90.0 1.9 collective-permute-start.4
  92.0 1.5 collective-permute-start.5
  94.8 4.4 collective-permute-done.5
  99.2 34.8 %add_reduce_fusion = (f32[128,64]{0,1:T(8,128)S(1)}, f32[128,64]{0,1:T(8,128)S(1)}, f32[128,8,128,64]{0,3,2,1:T(8,128)}) fusion(f32[64]{0:T(128)S(1)} %get-tuple-element.54, bf16[3,3,64,64]{3,2,1,0:T(8,128)(2,1)S(1)} %copy-done.12, bf16[128,10,1,64]{0,3,2,1:T(8,128)(2,1)S(1)} %collective-permute-done.5, bf16[128,1,128,64]{0,3,2,1:T(8,128)(2,1)} %copy-done.1, ...), kind=kOutput, calls=%fused_computation.4 | convolution fusion | flops 9739812864 | bytes 54993152 | tf_op jit(solution)/shard_map/conv_general_dilated | solution.py:46
  134.0 41.8 %psum.43 = f32[2,128,8]{1,2,0:T(8,128)S(1)} all-reduce(f32[2,128,8]{1,2,0:T(8,128)S(1)} %maximum_reduce_fusion.5), channel_id=1, replica_groups=mesh['batch'=1,'w'=2,'h'=4] {'h','w'}, use_global_device_ids=true, to_apply=%region_7.8 | all-reduce | flops 2048 | bytes 16384 | tf_op jit(solution)/shard_map/psum | solution.py:52
  175.9 14.3 %maximum_convert_fusion = bf16[128,8,128,64]{0,3,2,1:T(8,128)(2,1)S(1)} fusion(f32[128,8,128,64]{0,3,2,1:T(8,128)} %get-tuple-element.72, f32[128,64]{0,1:T(8,128)S(1)} %get-tuple-element.68, f32[128,64]{0,1:T(8,128)S(1)} %get-tuple-element.67, f32[64]{0:T(128)S(1)} %get-tuple-element.54), kind=kLoop, calls=%fused_computation | loop fusion | flops 41943040 | bytes 50397440 | tf_op jit(solution)/shard_map/convert_element_type | solution.py:42
  190.4 1.6 collective-permute-start.6
  192.0 3.6 collective-permute-done.6
  195.6 4.4 collective-permute-start.7
  200.0 2.6 collective-permute-done.7
  202.6 14.2 %add_reduce_fusion.3 = (f32[128,128]{1,0:T(8,128)S(1)}, f32[128,128]{1,0:T(8,128)S(1)}, f32[128,4,64,128]{3,0,2,1:T(8,128)}) fusion(f32[128]{0:T(128)S(1)} %get-tuple-element.51, bf16[3,3,64,128]{3,2,1,0:T(8,128)(2,1)S(1)} %copy-done.13, bf16[128,8,128,64]{0,3,2,1:T(8,128)(2,1)S(1)} %maximum_convert_fusion, ...), kind=kOutput, calls=%fused_computation.27 | convolution fusion | flops 4867604480 | bytes 36078080 | tf_op jit(solution)/shard_map/conv_general_dilated | solution.py:46
  217.1 47.1 %psum.44 = f32[2,128,8]{1,2,0:T(8,128)S(1)} all-reduce(f32[2,128,8]{1,2,0:T(8,128)S(1)} %maximum_reduce_fusion.2), channel_id=1, replica_groups=mesh['batch'=1,'w'=2,'h'=4] {'h','w'}, use_global_device_ids=true, to_apply=%region_11.12 | all-reduce | flops 2048 | bytes 16384 | tf_op jit(solution)/shard_map/psum | solution.py:52
  264.5 7.7 %maximum_convert_fusion.3 = bf16[128,4,64,128]{3,0,2,1:T(8,128)(2,1)S(1)} fusion(f32[128,4,64,128]{3,0,2,1:T(8,128)} %get-tuple-element.73, f32[128,128]{1,0:T(8,128)S(1)} %copy.41, f32[128,128]{1,0:T(8,128)S(1)} %copy.40, f32[128]{0:T(128)S(1)} %get-tuple-element.51), kind=kLoop, calls=%fused_computation.24 | loop fusion | flops 20971520 | bytes 25297408 | tf_op jit(solution)/shard_map/convert_element_type | solution.py:42
  272.8 1.4 collective-permute-start.8
  275.5 2.3 collective-permute-done.8
  277.9 4.8 collective-permute-done.9
  282.7 2.0 collective-permute-start.10
  286.0 1.8 collective-permute-done.10
  287.8 4.4 collective-permute-done.11
  292.3 22.4 %add_reduce_fusion.2 = (f32[128,128]{1,0:T(8,128)S(1)}, f32[128,128]{1,0:T(8,128)S(1)}, f32[128,4,64,128]{3,0,2,1:T(8,128)}) fusion(f32[128]{0:T(128)S(1)} %get-tuple-element.48, bf16[3,3,128,128]{3,2,1,0:T(8,128)(2,1)S(1)} %copy-done.11, bf16[128,6,1,128]{3,0,2,1:T(8,128)(2,1)S(1)} %collective-permute-done.11, ...), kind=kOutput, calls=%fused_computation.26 | convolution fusion | flops 9706373120 | bytes 30179840 | tf_op jit(solution)/shard_map/conv_general_dilated | solution.py:46
  314.9 41.8 %psum.45 = f32[2,128,8]{1,2,0:T(8,128)S(1)} all-reduce(f32[2,128,8]{1,2,0:T(8,128)S(1)} %maximum_reduce_fusion.3), channel_id=1, replica_groups=mesh['batch'=1,'w'=2,'h'=4] {'h','w'}, use_global_device_ids=true, to_apply=%region_15.16 | all-reduce | flops 2048 | bytes 16384 | tf_op jit(solution)/shard_map/psum | solution.py:52
  357.1 7.6 %maximum_convert_fusion.2 = bf16[128,4,64,128]{3,0,2,1:T(8,128)(2,1)S(1)} fusion(f32[128,4,64,128]{3,0,2,1:T(8,128)} %get-tuple-element.74, f32[128,128]{1,0:T(8,128)S(1)} %copy.45, f32[128,128]{1,0:T(8,128)S(1)} %copy.44, f32[128]{0:T(128)S(1)} %get-tuple-element.48), kind=kLoop, calls=%fused_computation.22 | loop fusion | flops 20971520 | bytes 25297408 | tf_op jit(solution)/shard_map/convert_element_type | solution.py:42
  364.9 1.6 collective-permute-start.12
  366.4 3.6 collective-permute-done.12
  370.1 4.6 collective-permute-start.13
  374.7 2.5 collective-permute-done.13
  377.2 8.0 %add_reduce_fusion.5 = (f32[128,256]{1,0:T(8,128)S(1)}, f32[128,256]{1,0:T(8,128)S(1)}, f32[128,2,32,256]{3,0,2,1:T(8,128)}) fusion(f32[256]{0:T(256)S(1)} %bitcast.206, bf16[3,3,128,256]{3,2,1,0:T(8,128)(2,1)S(1)} %copy-done.10, bf16[128,4,64,128]{3,0,2,1:T(8,128)(2,1)S(1)} %maximum_convert_fusion.2, ...), kind=kOutput, calls=%fused_computation.59 | convolution fusion | flops 4850810880 | bytes 19891200 | tf_op jit(solution)/shard_map/conv_general_dilated | solution.py:46
  385.5 46.9 %psum.46 = f32[2,128,8]{1,2,0:T(8,128)S(1)} all-reduce(f32[2,128,8]{1,2,0:T(8,128)S(1)} %maximum_reduce_fusion), channel_id=1, replica_groups=mesh['batch'=1,'w'=2,'h'=4] {'h','w'}, use_global_device_ids=true, to_apply=%region_19.20 | all-reduce | flops 2048 | bytes 16384 | tf_op jit(solution)/shard_map/psum | solution.py:52
  432.8 4.8 maximum_convert_fusion.5
  440.6 2.3 collective-permute-done.14
  443.0 4.8 collective-permute-done.15
  447.8 2.0 collective-permute-start.16
  451.1 2.5 collective-permute-done.16
  453.6 4.4 collective-permute-done.17
  458.1 12.1 %add_reduce_fusion.4 = (f32[128,256]{1,0:T(8,128)S(1)}, f32[128,256]{1,0:T(8,128)S(1)}, f32[128,2,32,256]{3,0,2,1:T(8,128)}) fusion(f32[256]{0:T(256)S(1)} %bitcast.204, bf16[3,3,256,256]{3,2,1,0:T(8,128)(2,1)S(1)} %copy-done, bf16[128,4,1,256]{3,0,2,1:T(8,128)(2,1)S(1)} %collective-permute-done.17, ...), kind=kOutput, calls=%fused_computation.58 | convolution fusion | flops 9689825280 | bytes 18744320 | tf_op jit(solution)/shard_map/conv_general_dilated | solution.py:46
  470.4 42.1 %psum.47 = f32[2,128,8]{1,2,0:T(8,128)S(1)} all-reduce(f32[2,128,8]{1,2,0:T(8,128)S(1)} %maximum_reduce_fusion.1), channel_id=1, replica_groups=mesh['batch'=1,'w'=2,'h'=4] {'h','w'}, use_global_device_ids=true, to_apply=%region_23.24 | all-reduce | flops 2048 | bytes 16384 | tf_op jit(solution)/shard_map/psum | solution.py:52
  512.8 4.8 maximum_convert_fusion.4
  517.7 4.5 copy.54
  (90 shorter events, 18.2 us)
Async XLA Ops:
  0.0 458.1 %copy-start = (bf16[3,3,256,256]{3,2,1,0:T(8,128)(2,1)S(1)}, bf16[3,3,256,256]{3,2,1,0:T(8,128)(2,1)}, u32[]{:S(2)}) copy-start(bf16[3,3,256,256]{3,2,1,0:T(8,128)(2,1)} %param.24) | copy-start | bytes 3538948
  0.0 16.2 %copy-start.6 = (f32[3,64]{1,0:T(4,128)S(1)}, f32[3,64]{1,0:T(4,128)}, u32[]{:S(2)}) copy-start(f32[3,64]{1,0:T(4,128)} %param.15) | copy-start | bytes 2308
  0.0 17.6 %copy-start.14 = (bf16[3,3,3,64]{3,2,1,0:T(4,128)(2,1)S(1)}, bf16[3,3,3,64]{3,2,1,0:T(4,128)(2,1)}, u32[]{:S(2)}) copy-start(bf16[3,3,3,64]{3,2,1,0:T(4,128)(2,1)} %param.14) | copy-start | bytes 10372
  7.2 3.9 collective-permute-start
  11.9 5.7 %collective-permute-start.1 = (bf16[128,17,1,3]{0,3,2,1:T(4,128)(2,1)S(1)}, bf16[128,17,1,3]{0,3,2,1:T(4,128)(2,1)S(1)}, u32[]{:S(2)}, u32[]{:S(2)}) collective-permute-start(bf16[128,17,1,3]{0,3,2,1:T(4,128)(2,1)S(1)} %pad_maximum_fusion.11), channel_id=1, source_target_pairs={{0,4},{1,5},{2,6},{3,7}} | collective-permute-start | bytes 39176 | tf_op jit(solution)/shard_map/ppermute | solution.py:17
  78.7 5.1 collective-permute-start.2
  80.1 13.3 %copy-start.7 = (f32[3,64]{1,0:T(4,128)S(1)}, f32[3,64]{1,0:T(4,128)}, u32[]{:S(2)}) copy-start(f32[3,64]{1,0:T(4,128)} %param.17) | copy-start | bytes 2308
  80.1 19.1 %copy-start.12 = (bf16[3,3,64,64]{3,2,1,0:T(8,128)(2,1)S(1)}, bf16[3,3,64,64]{3,2,1,0:T(8,128)(2,1)}, u32[]{:S(2)}) copy-start(bf16[3,3,64,64]{3,2,1,0:T(8,128)(2,1)} %param.16) | copy-start | bytes 221188
  80.1 8.6 %collective-permute-start.3 = (bf16[128,1,128,64]{0,3,2,1:T(8,128)(2,1)S(1)}, bf16[128,1,128,64]{0,3,2,1:T(8,128)(2,1)S(1)}, u32[]{:S(2)}, u32[]{:S(2)}) collective-permute-start(bf16[128,1,128,64]{0,3,2,1:T(8,128)(2,1)S(1)} %get-tuple-element.32), channel_id=1, source_target_pairs={{1,0},{2,1},{3,2},{5,4},{6,5},{7,6}} | collective-permute-start | bytes 6291464 | tf_op jit(solution)/shard_map/ppermute | solution.py:17
  88.7 1.3 copy-start.1
  90.0 4.8 collective-permute-start.4
  92.0 7.2 %collective-permute-start.5 = (bf16[128,10,1,64]{0,3,2,1:T(8,128)(2,1)S(1)}, bf16[128,10,1,64]{0,3,2,1:T(8,128)(2,1)S(1)}, u32[]{:S(2)}, u32[]{:S(2)}) collective-permute-start(bf16[128,10,1,64]{0,3,2,1:T(8,128)(2,1)S(1)} %get-tuple-element.30), channel_id=1, source_target_pairs={{4,0},{5,1},{6,2},{7,3}} | collective-permute-start | bytes 491528 | tf_op jit(solution)/shard_map/ppermute | solution.py:17
  99.2 76.6 %copy-start.4 = (f32[64]{0:T(128)S(1)}, f32[64]{0:T(128)}, u32[]{:S(2)}) copy-start(f32[64]{0:T(128)} %get-tuple-element.53) | copy-start | bytes 772
  99.2 76.6 %copy-start.5 = (f32[64]{0:T(128)S(1)}, f32[64]{0:T(128)}, u32[]{:S(2)}) copy-start(f32[64]{0:T(128)} %get-tuple-element.55) | copy-start | bytes 772
  190.4 9.6 %copy-start.8 = (f32[3,128]{1,0:T(4,128)S(1)}, f32[3,128]{1,0:T(4,128)}, u32[]{:S(2)}) copy-start(f32[3,128]{1,0:T(4,128)} %param.19) | copy-start | bytes 4612
  190.4 12.3 %copy-start.13 = (bf16[3,3,64,128]{3,2,1,0:T(8,128)(2,1)S(1)}, bf16[3,3,64,128]{3,2,1,0:T(8,128)(2,1)}, u32[]{:S(2)}) copy-start(bf16[3,3,64,128]{3,2,1,0:T(8,128)(2,1)} %param.18) | copy-start | bytes 442372
  190.4 5.2 collective-permute-start.6
  195.6 7.0 %collective-permute-start.7 = (bf16[128,9,1,64]{0,3,2,1:T(8,128)(2,1)S(1)}, bf16[128,9,1,64]{0,3,2,1:T(8,128)(2,1)S(1)}, u32[]{:S(2)}, u32[]{:S(2)}) collective-permute-start(bf16[128,9,1,64]{0,3,2,1:T(8,128)(2,1)S(1)} %pad_maximum_fusion.10), channel_id=1, source_target_pairs={{0,4},{1,5},{2,6},{3,7}} | collective-permute-start | bytes 442376 | tf_op jit(solution)/shard_map/ppermute | solution.py:17
  272.2 13.8 %copy-start.9 = (f32[3,128]{1,0:T(4,128)S(1)}, f32[3,128]{1,0:T(4,128)}, u32[]{:S(2)}) copy-start(f32[3,128]{1,0:T(4,128)} %param.21) | copy-start | bytes 4612
  272.2 20.0 %copy-start.11 = (bf16[3,3,128,128]{3,2,1,0:T(8,128)(2,1)S(1)}, bf16[3,3,128,128]{3,2,1,0:T(8,128)(2,1)}, u32[]{:S(2)}) copy-start(bf16[3,3,128,128]{3,2,1,0:T(8,128)(2,1)} %param.20) | copy-start | bytes 884740
  272.8 5.1 collective-permute-start.8
  274.2 8.4 %collective-permute-start.9 = (bf16[128,1,64,128]{3,0,2,1:T(8,128)(2,1)S(1)}, bf16[128,1,64,128]{3,0,2,1:T(8,128)(2,1)S(1)}, u32[]{:S(2)}, u32[]{:S(2)}) collective-permute-start(bf16[128,1,64,128]{3,0,2,1:T(8,128)(2,1)S(1)} %get-tuple-element.38), channel_id=1, source_target_pairs={{1,0},{2,1},{3,2},{5,4},{6,5},{7,6}} | collective-permute-start | bytes 6291464 | tf_op jit(solution)/shard_map/ppermute | solution.py:17
  282.7 5.1 collective-permute-start.10
  284.7 7.6 %collective-permute-start.11 = (bf16[128,6,1,128]{3,0,2,1:T(8,128)(2,1)S(1)}, bf16[128,6,1,128]{3,0,2,1:T(8,128)(2,1)S(1)}, u32[]{:S(2)}, u32[]{:S(2)}) collective-permute-start(bf16[128,6,1,128]{3,0,2,1:T(8,128)(2,1)S(1)} %get-tuple-element.34), channel_id=1, source_target_pairs={{4,0},{5,1},{6,2},{7,3}} | collective-permute-start | bytes 589832 | tf_op jit(solution)/shard_map/ppermute | solution.py:17
  364.7 10.0 %copy-start.2 = (f32[3,256]{1,0:T(4,128)S(1)}, f32[3,256]{1,0:T(4,128)}, u32[]{:S(2)}) copy-start(f32[3,256]{1,0:T(4,128)} %param.23) | copy-start | bytes 9220
  364.7 12.5 %copy-start.10 = (bf16[3,3,128,256]{3,2,1,0:T(8,128)(2,1)S(1)}, bf16[3,3,128,256]{3,2,1,0:T(8,128)(2,1)}, u32[]{:S(2)}) copy-start(bf16[3,3,128,256]{3,2,1,0:T(8,128)(2,1)} %param.22) | copy-start | bytes 1769476
  364.9 5.2 collective-permute-start.12
  370.1 7.2 %collective-permute-start.13 = (bf16[128,5,1,128]{3,0,2,1:T(8,128)(2,1)S(1)}, bf16[128,5,1,128]{3,0,2,1:T(8,128)(2,1)S(1)}, u32[]{:S(2)}, u32[]{:S(2)}) collective-permute-start(bf16[128,5,1,128]{3,0,2,1:T(8,128)(2,1)S(1)} %pad_maximum_fusion.6), channel_id=1, source_target_pairs={{0,4},{1,5},{2,6},{3,7}} | collective-permute-start | bytes 491528 | tf_op jit(solution)/shard_map/ppermute | solution.py:17
  437.6 13.5 %copy-start.3 = (f32[3,256]{1,0:T(4,128)S(1)}, f32[3,256]{1,0:T(4,128)}, u32[]{:S(2)}) copy-start(f32[3,256]{1,0:T(4,128)} %param.25) | copy-start | bytes 9220
  437.9 5.1 collective-permute-start.14
  439.3 8.4 %collective-permute-start.15 = (bf16[128,1,32,256]{3,0,2,1:T(8,128)(2,1)S(1)}, bf16[128,1,32,256]{3,0,2,1:T(8,128)(2,1)S(1)}, u32[]{:S(2)}, u32[]{:S(2)}) collective-permute-start(bf16[128,1,32,256]{3,0,2,1:T(8,128)(2,1)S(1)} %get-tuple-element.40), channel_id=1, source_target_pairs={{1,0},{2,1},{3,2},{5,4},{6,5},{7,6}} | collective-permute-start | bytes 6291464 | tf_op jit(solution)/shard_map/ppermute | solution.py:17
  447.8 5.8 %collective-permute-start.16 = (bf16[128,4,1,256]{3,0,2,1:T(8,128)(2,1)S(1)}, bf16[128,4,1,256]{3,0,2,1:T(8,128)(2,1)S(1)}, u32[]{:S(2)}, u32[]{:S(2)}) collective-permute-start(bf16[128,4,1,256]{3,0,2,1:T(8,128)(2,1)S(1)} %get-tuple-element.35), channel_id=1, source_target_pairs={{0,4},{1,5},{2,6},{3,7}} | collective-permute-start | bytes 786440 | tf_op jit(solution)/shard_map/ppermute | solution.py:17
  449.8 8.3 %collective-permute-start.17 = (bf16[128,4,1,256]{3,0,2,1:T(8,128)(2,1)S(1)}, bf16[128,4,1,256]{3,0,2,1:T(8,128)(2,1)S(1)}, u32[]{:S(2)}, u32[]{:S(2)}) collective-permute-start(bf16[128,4,1,256]{3,0,2,1:T(8,128)(2,1)S(1)} %get-tuple-element.36), channel_id=1, source_target_pairs={{4,0},{5,1},{6,2},{7,3}} | collective-permute-start | bytes 786440 | tf_op jit(solution)/shard_map/ppermute | solution.py:17
where the time goes:
time: 530 us; the launch traced here: 523 us
  blocking collectives  249 us (47%)
  matrix products  108 us (20%)
  other arithmetic  55.3 us (10%)
  waiting for transfers between devices  54.7 us (10%)
  starting transfers between devices  37.3 us (7%)
  local copies, waits for them, and re-layouts  17.2 us (3%)
    psum x6, blocking collectives, conv_norm(): totals = lax.psum(part_sums, ('h', 'w'))  249 us
    conv_general_dilated x6, matrix products, conv_norm(): lax.conv_general_dilated(padded, kernel, (stride, stride), 'VALID', dimen...  108 us
    ppermute x18, waiting for transfers between devices, shift_in(): return lax.ppermute(piece, axis_name, send_pairs)  54.7 us
    convert_element_type x6, other arithmetic, norm_apply(): jax.nn.relu(summed * chan_scale[:, None, None, :] + chan_shift[:, None, N...  53.5 us
    ppermute x18, starting transfers between devices, shift_in(): return lax.ppermute(piece, axis_name, send_pairs)  37.3 us
  transfers between devices with their start and end apart: 18, of which 18 were waited for; matrix products, arithmetic and copies ran while one was open for 0% of the time, Pallas kernels for 0%

commit v1 on v0

v1 whole, which is shorter than its diff:
```python
import jax
import jax.numpy as jnp
from jax import lax
from jax.experimental import pallas as pl
from jax.experimental.pallas import tpu as pltpu
from jax.sharding import PartitionSpec as P

NORM_EPS = 1e-5
BF = jnp.bfloat16
F32 = jnp.float32
PAIR, SUB, TILE, LANES, WIDE = 2, 8, 16, 128, 256
PEERS, GROUPS, HALVES = 8, 8, 2
C1, C2, C3 = 64, 128, 256
PHASES, PIECE_ROWS, PIECE_COLS = 5, 48, 256
AREAS = (32 * 256, 16 * 128, 8 * 64)
MESH = pl.DeviceIdType.MESH
LOW, HIGH = slice(None, LANES), slice(LANES, None)


def dot(lhs, rhs):
    return jnp.dot(lhs, rhs, preferred_element_type=F32)


def iota(shape, dim):
    return lax.broadcasted_iota(jnp.int32, shape, dim)


def one_hot(mask):
    return jnp.where(mask, 1.0, 0.0).astype(BF)


def join(parts, axis=0):
    return jnp.concatenate(parts, axis=axis)


def rows_of(ref, index, first, count):
    return ref[index, first:first + count].reshape(count * TILE, ref.shape[-1])


def tiles_of(block):
    return block.reshape(-1, TILE, WIDE)


def lane_half(ref, half):
    return ref.at[..., LOW] if half == 0 else ref.at[..., HIGH]


def expand_first(down1, taps, w1):
    taps[...] = jnp.zeros(taps.shape, F32)
    for dy in range(3):
        for dx in range(3):
            taps[pl.ds(9 * dy + 3 * dx, 3), :] = down1[dy, dx].astype(F32)
    source = taps[...].astype(BF)
    row, tap = iota((WIDE, 32), 0), iota((WIDE, 32), 1)
    colour_phase = (row % LANES) // SUB
    colour, phase = colour_phase // PHASES, colour_phase % PHASES
    line = SUB * (row // LANES) + row % SUB
    for o in range(HALVES):
        lanes = []
        for cp in range(HALVES):
            for rp in range(HALVES):
                dy, dx = line - 7 - 4 * o - 2 * rp, phase - 2 * cp
                inside = (dy >= 0) & (dy < 3) & (dx >= 0) & (dx < 3) & (colour < 3)
                lanes.append(dot(one_hot(inside & (tap == 9 * dy + 3 * dx + colour)), source))
        w1[o] = join(lanes, 1).astype(BF)


def expand_refine1(refine1, wr1):
    blank = jnp.zeros((C1, C1), BF)
    wr1[...] = jnp.zeros(wr1.shape, BF)
    for dx in range(3):
        for y in range(4):
            pair = join([refine1[y, dx] if y < 3 else blank, refine1[y - 1, dx] if y else blank], 1)
            for cp in range(HALVES):
                lane_half(wr1, cp)[pl.ds(((dx + cp) * 4 + y) * C1, C1), :] = pair


def expand_rows(kernel, out, shift, order):
    depth = kernel.shape[2]
    out[...] = jnp.zeros(out.shape, BF)
    for dy in range(3):
        for dx in range(3):
            for r in range(HALVES):
                lane_half(out, r)[pl.ds(order(dy + shift * r, dx) * depth, depth), :] = kernel[dy, dx]


def encoder_kernel(image, down1, v1, refine1, v2, down2, v3, refine2, v4, wd3, v5, wr3, v6, out, inbuf, outbuf, in_send, in_recv, out_send, out_recv, taps,
                   vecs, w1, wr1, wd2, wr2, perm, gmat, af, bs, abuf, y1e, y1o, z1e, z1o, y2, z2e, z2o, y3, obuf):
    group = pl.program_id(0)
    me = 2 * lax.axis_index("h") + lax.axis_index("w")

    def peer(k):
        return lax.rem(me + k, PEERS)

    def device(index):
        return {"h": index // 2, "w": lax.rem(index, 2)}

    def images(index, g):
        return pl.ds(index * PAIR * GROUPS + PAIR * g, PAIR)

    def send_in(g, to, sender):
        return pltpu.make_async_remote_copy(image.at[images(to, g)], inbuf.at[g, sender], in_send.at[g, to], in_recv.at[g, sender], device_id=device(to), device_id_type=MESH)

    def keep_in(g):
        return pltpu.make_async_copy(image.at[images(me, g)], inbuf.at[g, me], in_recv.at[g, me])

    def send_out(g, to, sender):
        return pltpu.make_async_remote_copy(outbuf.at[g, to], out.at[images(sender, g)], out_send.at[g, to], out_recv.at[g, sender], device_id=device(to), device_id_type=MESH)

    def keep_out(g):
        return pltpu.make_async_copy(outbuf.at[g, me], out.at[images(me, g)], out_recv.at[g, me])

    def start_out(g):
        for k in range(1, PEERS):
            send_out(g, peer(k), me).start()
        keep_out(g).start()

    @pl.when(group == 0)
    def _():
        barrier = pltpu.get_barrier_semaphore()
        for k in range(1, PEERS):
            pl.semaphore_signal(barrier, inc=1, device_id=device(peer(k)), device_id_type=MESH)
        pl.semaphore_wait(barrier, PEERS - 1)

        def begin(g, _):
            keep_in(g).start()
            for k in range(1, PEERS):
                send_in(g, peer(k), me).start()
            return 0

        lax.fori_loop(0, GROUPS, begin, 0)

        expand_first(down1, taps, w1)
        expand_refine1(refine1, wr1)
        expand_rows(down2, wd2, 2, lambda y, x: 6 * x + y)
        expand_rows(refine2, wr2, 1, lambda y, x: 3 * y + x)
        for i, ref in enumerate((v1, v2, v3, v4, v5, v6)):
            vecs[i] = join([ref[...]] * (WIDE // ref.shape[1]), 1)
        row, lane = iota((2 * WIDE, LANES), 0), iota((2 * WIDE, LANES), 1)
        for d in range(PHASES):
            perm[:, d * LANES:(d + 1) * LANES] = one_hot(row == 4 * ((lane % SUB) * TILE + lane // SUB) + d - 1)
        row, lane = iota((WIDE, WIDE), 0), iota((WIDE, WIDE), 1)
        for g, rep in enumerate((C1, C2, C3)):
            gmat[g] = one_hot((row % rep) // (rep // SUB) == (lane % rep) // (rep // SUB))
        for ref in (y1e, y1o, y2, y3, z2e, z2o, bs):
            ref[0] = jnp.zeros(ref.shape[1:], BF)
        for ref in (y1e, y1o, y2, y3):
            ref[ref.shape[0] - 1] = jnp.zeros(ref.shape[1:], BF)

    @pl.when(group > 0)
    def _():
        start_out(group - 1)

    keep_in(group).wait()
    for k in range(1, PEERS):
        send_in(group, peer(k), peer(k)).wait_recv()

    strip = iota((SUB, LANES), 0)
    not_first = jnp.where(strip == 0, 0.0, 1.0)
    not_last = jnp.where(strip == SUB - 1, 0.0, 1.0)

    def from_left(tile):
        return join([pltpu.roll(tile[SUB * e:SUB * e + SUB], 1, 0) * not_first for e in range(PAIR)]).astype(BF)

    def from_right(tile):
        return join([pltpu.roll(tile[SUB * e:SUB * e + SUB], SUB - 1, 0) * not_last for e in range(PAIR)]).astype(BF)

    def moments(acc, carry):
        tiles = tiles_of(acc)
        return carry[0] + jnp.sum(tiles, axis=0), carry[1] + jnp.sum(tiles * tiles, axis=0)

    def conv(trips, body):
        zeros = jnp.zeros((TILE, WIDE), F32)
        return lax.fori_loop(0, trips, body, (zeros, zeros))

    def finalize(layer, sums):
        rep = (C1, C2, C3)[layer // 2]
        area = AREAS[layer // 2]
        per_strip = area * rep / (WIDE * SUB)
        count = float(area * rep // SUB)
        bias, gain, offset = vecs[layer, 0:1, :], vecs[layer, 1:2, :], vecs[layer, 2:3, :]
        first = sums[0] + per_strip * bias
        second = sums[1] + 2.0 * bias * sums[0] + per_strip * bias * bias
        rest = join([first, second])
        parts = []
        for _ in range(3):
            parts.append(rest.astype(BF))
            rest = rest - parts[-1].astype(F32)
        grouped = jnp.sum(dot(join(parts), gmat[layer // 2]).reshape(3, 2 * PAIR, SUB, WIDE), axis=0)
        grouped = jnp.sum(grouped, axis=1, keepdims=True) / count
        scales, shifts = [], []
        for e in range(PAIR):
            mean, square = grouped[e], grouped[PAIR + e]
            scale = lax.rsqrt(jnp.maximum(square - mean * mean, 0.0) + NORM_EPS) * gain
            scales.append(jnp.broadcast_to(scale, (SUB, WIDE)))
            shifts.append(jnp.broadcast_to(offset + (bias - mean) * scale, (SUB, WIDE)))
        return join(scales), join(shifts)

    def apply(block, norm):
        return jnp.maximum(block * norm[0] + norm[1], 0.0)

    for e in range(PAIR):
        sides = [join([inbuf[group, HALVES * hh + half, e] for hh in range(4)]) for half in range(HALVES)]
        af[e] = dot(join(sides, 1), perm[...]).reshape(af.shape[1:])

    def im2col(k, _):
        pair = []
        for e in range(PAIR):
            rows = []
            for c in range(3):
                block = af[e, (k // 2) * 6 + c * 2 + lax.rem(k, 2)]
                rows += [block[:, d * LANES:(d + 1) * LANES] for d in range(PHASES)]
            rows.append(jnp.zeros((SUB, LANES), F32))
            pair.append(join(rows).T.reshape(TILE, SUB, LANES))
        bs[k + 1] = join(pair, 1).astype(BF)
        return 0

    lax.fori_loop(0, SUB, im2col, 0)

    def conv_down1(k, carry):
        lhs = join([rows_of(bs, k, 0, TILE), rows_of(bs, k + 1, 0, TILE)], 1)
        for o in range(HALVES):
            acc = dot(lhs, w1[o])
            abuf[2 * k + o] = tiles_of(acc)
            carry = moments(acc, carry)
        return carry

    norm = finalize(0, conv(SUB, conv_down1))

    def norm1(i, _):
        val = apply(abuf[i], norm)
        y1e[i + 1, 0:TILE] = val[..., LOW].astype(BF)
        y1o[i + 1, 1:] = val[..., HIGH].astype(BF)
        y1o[i + 1, 0] = from_left(val[TILE - 1][:, HIGH])
        y1e[i + 1, TILE] = from_right(val[0][:, LOW])
        return 0

    lax.fori_loop(0, TILE, norm1, 0)

    def refine1_lhs(rows):
        tiles = []
        for first in range(2):
            for ref in (y1o, y1e):
                for a in range(2):
                    tiles.append(join([rows_of(ref, i + a, first, TILE) for i in rows]))
        return join(tiles, 1)

    upper = (iota((1, WIDE), 1) % LANES) < C1
    keep = {0: jnp.where(upper, 0.0, 1.0), TILE: jnp.where(upper, 1.0, 0.0)}

    def conv_refine1(t, carry):
        rows = [1 + 3 * t + r for r in range(3)]
        acc = dot(refine1_lhs(rows), wr1[...])
        for r, i in enumerate(rows):
            abuf[i] = tiles_of(acc)[r * TILE:(r + 1) * TILE]
        return moments(acc, carry)

    carry = conv(5, conv_refine1)
    acc = dot(refine1_lhs(list(keep)), wr1[...])
    for part, i in enumerate(keep):
        edge = acc[part * WIDE:(part + 1) * WIDE] * keep[i]
        abuf[i] = tiles_of(edge)
        carry = moments(edge, carry)
    norm = finalize(1, carry)

    def norm2_row(i, val):
        z1e[i] = val[..., LOW].astype(BF)
        z1o[i, 1:] = val[..., HIGH].astype(BF)
        z1o[i, 0] = from_left(val[TILE - 1][:, HIGH])

    def norm2(i, _):
        norm2_row(i, apply(abuf[i], norm))
        return 0

    lax.fori_loop(1, TILE, norm2, 0)
    for i in keep:
        norm2_row(i, apply(abuf[i], norm) * keep[i])

    def put_pair(acc, t):
        half = acc.shape[0] // 2
        abuf[2 * t] = tiles_of(acc[:half])
        abuf[2 * t + 1] = tiles_of(acc[half:])

    def conv_down2(t, carry):
        tiles = []
        for ref, first in ((z1o, 0), (z1e, 0), (z1o, 1)):
            for a in range(3):
                tiles.append(join([rows_of(ref, 4 * t + 2 * u + a, first, TILE) for u in range(2)]))
        acc = dot(join(tiles, 1), wd2[...])
        put_pair(acc, t)
        return moments(acc, carry)

    norm = finalize(2, conv(4, conv_down2))

    def norm3(u, _):
        val = apply(abuf[u], norm)
        for v, part in enumerate((LOW, HIGH)):
            row = val[..., part]
            y2[2 * u + v + 1, 1:TILE + 1] = row.astype(BF)
            y2[2 * u + v + 1, 0] = from_left(row[TILE - 1])
            y2[2 * u + v + 1, TILE + 1] = from_right(row[0])
        return 0

    lax.fori_loop(0, SUB, norm3, 0)

    def conv_refine2(t, carry):
        tiles = []
        for a in range(4):
            for b in range(3):
                tiles.append(join([rows_of(y2, 4 * t + 2 * u + a, b, TILE) for u in range(2)]))
        acc = dot(join(tiles, 1), wr2[...])
        put_pair(acc, t)
        return moments(acc, carry)

    norm = finalize(3, conv(4, conv_refine2))

    def norm4(u, _):
        for q in range(TILE):
            val = apply(abuf[u, q], norm)
            for v, part in enumerate((LOW, HIGH)):
                if q % 2:
                    z2o[2 * u + v + 1, q // 2 + 1] = val[:, part].astype(BF)
                else:
                    z2e[2 * u + v + 1, q // 2] = val[:, part].astype(BF)
                if q == TILE - 1:
                    z2o[2 * u + v + 1, 0] = from_left(val[:, part])
        return 0

    lax.fori_loop(0, SUB, norm4, 0)

    def conv_down3(t, carry):
        tiles = []
        for a in range(3):
            for ref, first in ((z2o, 0), (z2e, 0), (z2o, 1)):
                tiles.append(join([rows_of(ref, 8 * t + 2 * p + a, first, SUB) for p in range(4)]))
        acc = dot(join(tiles, 1), wd3[...])
        put_pair(acc, t)
        return moments(acc, carry)

    norm = finalize(4, conv(2, conv_down3))

    def norm5(u, _):
        val = apply(abuf[u], norm)
        for v in range(2):
            row = val[SUB * v:SUB * v + SUB]
            y3[2 * u + v + 1, 1:SUB + 1] = row.astype(BF)
            y3[2 * u + v + 1, 0] = join([from_left(row[SUB - 1][:, part]) for part in (LOW, HIGH)], 1)
            y3[2 * u + v + 1, SUB + 1] = join([from_right(row[0][:, part]) for part in (LOW, HIGH)], 1)
        return 0

    lax.fori_loop(0, 4, norm5, 0)

    def conv_refine3(t, carry):
        tiles = []
        for a in range(3):
            for b in range(3):
                tiles.append(join([rows_of(y3, 4 * t + p + a, b, SUB) for p in range(4)]))
        acc = dot(join(tiles, 1), wr3[...])
        put_pair(acc, t)
        return moments(acc, carry)

    norm = finalize(5, conv(2, conv_refine3))

    def norm6(u, _):
        val = apply(abuf[u], norm)
        for v in range(2):
            for e in range(PAIR):
                for h, part in enumerate((LOW, HIGH)):
                    for q in range(SUB):
                        obuf[v, e, h, pl.ds(q, SUB, SUB), :] = val[SUB * v + q, SUB * e:SUB * e + SUB, part]
                    for w in range(HALVES):
                        outbuf[group, 2 * u + w, e, v, :, part] = obuf[v, e, h, 32 * w:32 * w + 32].astype(BF)
        return 0

    lax.fori_loop(0, 4, norm6, 0)

    @pl.when(group == GROUPS - 1)
    def _():
        def sent(g, _):
            for k in range(1, PEERS):
                send_in(g, peer(k), me).wait_send()
            return 0

        lax.fori_loop(0, GROUPS, sent, 0)
        start_out(group)

        def done(g, _):
            for k in range(1, PEERS):
                send_out(g, peer(k), me).wait_send()
                send_out(g, peer(k), peer(k)).wait_recv()
            keep_out(g).wait()
            return 0

        lax.fori_loop(0, GROUPS, done, 0)


def solution(mesh):
    act_spec = P("batch", "h", "w")
    sems = pltpu.SemaphoreType.DMA((GROUPS, PEERS))
    scratch = [
        ((GROUPS, PEERS, PAIR, PIECE_ROWS, PIECE_COLS), BF), ((GROUPS, PEERS, PAIR, 2, 32, WIDE), BF), None, None, None, None, ((32, C1), F32),
        ((6, 3, WIDE), F32), ((2, WIDE, WIDE), BF), ((1024, WIDE), BF), ((1152, WIDE), BF), ((1536, WIDE), BF), ((512, 640), BF), ((3, WIDE, WIDE), BF),
        ((PAIR, 24, SUB, 640), F32), ((9, TILE, TILE, LANES), BF), ((17, TILE, TILE, WIDE), F32),
        ((18, 17, TILE, LANES), BF), ((18, 17, TILE, LANES), BF), ((17, 16, TILE, LANES), BF), ((17, 17, TILE, LANES), BF),
        ((18, 18, TILE, LANES), BF), ((17, 8, TILE, LANES), BF), ((17, 9, TILE, LANES), BF), ((10, 10, TILE, WIDE), BF), ((2, PAIR, 2, 64, LANES), F32),
    ]

    def local_forward(tile, *params):
        planes = tile.transpose(0, 3, 1, 2).reshape(-1, PIECE_ROWS, PIECE_COLS)
        params = list(params)
        params[8], params[10] = params[8].reshape(-1, WIDE), params[10].reshape(-1, WIDE)
        return pl.pallas_call(
            encoder_kernel,
            grid=(GROUPS,),
            out_shape=jax.ShapeDtypeStruct((128, 2, 32, WIDE), BF),
            in_specs=[pl.BlockSpec(memory_space=pl.ANY)] + [pl.BlockSpec(memory_space=pltpu.VMEM)] * 12,
            out_specs=pl.BlockSpec(memory_space=pl.ANY),
            scratch_shapes=[sems if entry is None else pltpu.VMEM(*entry) for entry in scratch],
            compiler_params=pltpu.CompilerParams(vmem_limit_bytes=60 * 1024 * 1024, collective_id=0, has_side_effects=True),
            name="encoder",
        )(planes, *params)

    return jax.shard_map(local_forward, mesh=mesh, in_specs=(act_spec,) + (P(),) * 12, out_specs=act_spec, check_vma=False)
```

time: 530 us -> 163 us (0.31); the launches traced: 523 us -> 163 us
  blocking collectives: 249 us -> 0 us
  Pallas kernels: 0 us -> 158 us
  matrix products: 108 us -> 0 us
  other arithmetic: 55.3 us -> 0 us
  waiting for transfers between devices: 54.7 us -> 0 us
  starting transfers between devices: 37.3 us -> 0 us
  local copies, waits for them, and re-layouts: 17.2 us -> 5.04 us
    psum x6 -> x0, blocking collectives: 249 us -> none  [conv_norm(): totals = lax.psum(part_sums, ('h', 'w'))]
    pallas_call x0 -> x1, Pallas kernels: none -> 158 us  [local_forward(): pl.pallas_call(encoder_kernel, grid=(GROUPS,), out_shape=jax.ShapeDtypeSt...]
    conv_general_dilated x6 -> x0, matrix products: 108 us -> none  [conv_norm(): lax.conv_general_dilated(padded, kernel, (stride, stride), 'VALID', dimen...]
    ppermute x18 -> x0, waiting for transfers between devices: 54.7 us -> none  [shift_in(): return lax.ppermute(piece, axis_name, send_pairs)]
    convert_element_type x6 -> x0, other arithmetic: 53.5 us -> none  [norm_apply(): jax.nn.relu(summed * chan_scale[:, None, None, :] + chan_shift[:, None, N...]
    ppermute x18 -> x0, starting transfers between devices: 37.3 us -> none  [shift_in(): return lax.ppermute(piece, axis_name, send_pairs)]
  transfers between devices with their start and end apart: 18 -> 0, of which waited for: 18 -> 0; matrix products, arithmetic and copies ran while one was open for 0% -> 0% of each run, Pallas kernels for 0% -> 0%
where the time goes in v1:
time: 163 us
  Pallas kernels  158 us (97%)
  local copies, waits for them, and re-layouts  5.04 us (3%)
    pallas_call x1, Pallas kernels, local_forward(): pl.pallas_call(encoder_kernel, grid=(GROUPS,), out_shape=jax.ShapeDtypeSt...  158 us
    unnamed x1, local copies, waits for them, and re-layouts  5.04 us

profile of v1, /device:TPU:0, one launch (start us, length us, event | category | flops | bytes accessed | tf_op | source)
XLA Modules:
  0.0 162.8 jit_solution(16912802734737511395)
XLA Ops:
  0.0 157.7 %encoder.1 = bf16[128,2,32,256]{3,2,1,0:T(8,128)(2,1)} custom-call(bf16[128,48,256]{2,1,0:T(8,128)(2,1)} %bitcast.5, bf16[3,3,3,64]{3,2,1,0:T(4,128)(2,1)} %down1.1, f32[3,64]{1,0:T(4,128)} %v1.1, bf16[3,3,64,64]{3,2,1,0:T(8,128)(2,1)} %refine1.1, f32[3,64]{1,0:T(4,128)} %v2.1, bf16[3,3,64,128]{3,2,1,0:T(8,128)(2,1)} %down2.1, f32[3,128]{1,0:T(4,128)} %v3.1, ...), custom_call_target="tpu_custom_call" | custom-call | tf_op jit(solution)/shard_map/encoder/pallas_call | solution.py:412
  157.7 5.0 %copy.15 = bf16[128,2,32,256]{3,2,1,0:T(8,128)(2,1)} copy(bf16[128,2,32,256]{3,2,1,0:T(8,128)(2,1)} %encoder.1) | data formatting | bytes 8388608

commit v2 on v0

v2 whole, which is shorter than its diff:
```python
import jax
import jax.numpy as jnp
from jax import lax
from jax.experimental import pallas as pl
from jax.experimental.pallas import tpu as pltpu
from jax.sharding import PartitionSpec as P

NORM_EPS = 1e-5
BF = jnp.bfloat16
F32 = jnp.float32
PAIR, SUB, TILE, LANES, WIDE, UNIT = 2, 8, 16, 128, 256, 128
CHUNK = 4
PEERS, GROUPS, HALVES = 8, 8, 2
C1, C2, C3 = 64, 128, 256
PHASES, PIECE_ROWS, PIECE_COLS = 5, 48, 256
AREAS = (32 * 256, 16 * 128, 8 * 64)
MESH = pl.DeviceIdType.MESH
LOW, HIGH = slice(None, LANES), slice(LANES, None)


def iota(shape, dim):
    return lax.broadcasted_iota(jnp.int32, shape, dim)


def one_hot(mask):
    return jnp.where(mask, 1.0, 0.0).astype(BF)


def join(parts, axis=0):
    return jnp.concatenate(parts, axis=axis)


def side_by_side(parts):
    return jnp.concatenate(parts, axis=1)


def rows_of(ref, index, first, count):
    return ref[index, first:first + count].reshape(count * TILE, ref.shape[-1])


def dot(lhs, rhs):
    return jnp.dot(lhs, rhs, preferred_element_type=F32)


def lane_half(ref, half):
    return ref.at[..., LOW] if half == 0 else ref.at[..., HIGH]


def expand_first(down1, taps, w1):
    taps[...] = jnp.zeros(taps.shape, F32)
    for dy in range(3):
        for dx in range(3):
            taps[pl.ds(9 * dy + 3 * dx, 3), :] = down1[dy, dx].astype(F32)
    source = taps[...].astype(BF)
    row, tap = iota((WIDE, 32), 0), iota((WIDE, 32), 1)
    colour_phase = (row % LANES) // SUB
    colour, phase = colour_phase // PHASES, colour_phase % PHASES
    line = SUB * (row // LANES) + row % SUB
    for o in range(HALVES):
        lanes = []
        for cp in range(HALVES):
            for rp in range(HALVES):
                dy, dx = line - 7 - 4 * o - 2 * rp, phase - 2 * cp
                inside = (dy >= 0) & (dy < 3) & (dx >= 0) & (dx < 3) & (colour < 3)
                lanes.append(dot(one_hot(inside & (tap == 9 * dy + 3 * dx + colour)), source))
        w1[:, o * WIDE:(o + 1) * WIDE] = side_by_side(lanes).astype(BF)


def expand_refine1(refine1, wr1):
    blank = jnp.zeros((C1, C1), BF)
    wr1[...] = jnp.zeros(wr1.shape, BF)
    for dx in range(3):
        for y in range(4):
            pair = side_by_side([refine1[y, dx] if y < 3 else blank, refine1[y - 1, dx] if y else blank])
            for cp in range(HALVES):
                lane_half(wr1, cp)[pl.ds(((y // 2 * 4 + dx + cp) * 2 + y % 2) * C1, C1), :] = pair


def expand_rows(kernel, out, shift, order):
    depth = kernel.shape[2]
    out[...] = jnp.zeros(out.shape, BF)
    for dy in range(3):
        for dx in range(3):
            for r in range(HALVES):
                lane_half(out, r)[pl.ds(order(dy + shift * r, dx) * depth, depth), :] = kernel[dy, dx]


def from_left(tile, strip):
    return jnp.where(strip == 0, 0.0, pltpu.roll(tile, 1, 0)).astype(BF)


def from_right(tile, strip):
    return jnp.where(strip == TILE - 1, 0.0, pltpu.roll(tile, TILE - 1, 0)).astype(BF)


class Stream:
    def __init__(self, params, buffers, put):
        self.put = put
        self.vecs, self.gmat, self.w1, self.wr1, self.wd2, self.wr2, self.wd3, self.wr3 = params
        self.bs, self.abuf, self.y1e, self.y1o, self.z1e, self.z1o, self.y2, self.z2e, self.z2o, self.y3, self.obuf, self.sums, self.norm = buffers
        self.strip = iota((TILE, LANES), 0)
        upper = (iota((1, WIDE), 1) % LANES) < C1
        self.keep = {0: jnp.where(upper, 0.0, 1.0), TILE: jnp.where(upper, 1.0, 0.0)}


    def lhs0(self, unit, step):
        return side_by_side([rows_of(self.bs, unit + n, 0, SUB) for n in range(2)])

    def lhs1(self, unit, step):
        return side_by_side([rows_of(ref, unit + step // 2, step % 2, SUB) for ref in (self.y1o, self.y1e)])

    def ninth(self, tile, step):
        return side_by_side([tile(2 * step), tile(2 * step + 1)]) if step < 4 else tile(2 * step)

    def lhs2(self, unit, step):
        taps = ((self.z1o, 0), (self.z1e, 0), (self.z1o, 1))

        def tile(n):
            ref, first = taps[n // 3]
            return rows_of(ref, 2 * unit + n % 3, first, SUB)

        return self.ninth(tile, step)

    def lhs3(self, unit, step):
        return side_by_side([rows_of(self.y2, 2 * unit + n // 3, n % 3, SUB) for n in (2 * step, 2 * step + 1)])

    def lhs4(self, unit, step):
        taps = ((self.z2o, 0), (self.z2e, 0), (self.z2o, 1))

        def tile(n):
            ref, first = taps[n % 3]
            return join([rows_of(ref, 2 * (2 * unit + p) + n // 3, first, 4) for p in range(2)])

        return self.ninth(tile, step)

    def lhs5(self, unit, step):
        return join([rows_of(self.y3, 2 * unit + p + step // 3, step % 3, 4) for p in range(2)])

    def finish(self, layer, unit, val):
        if layer == 1 and unit in self.keep:
            val = val * self.keep[unit]
        tiles = val.reshape(SUB, TILE, WIDE)
        self.abuf[unit] = tiles
        self.total[0] += jnp.sum(tiles, axis=0)
        self.total[1] += jnp.sum(tiles * tiles, axis=0)

    def conv(self, layer):
        lhs = (self.lhs0, self.lhs1, self.lhs2, self.lhs3, self.lhs4, self.lhs5)[layer]
        steps, ref, count = ((1, self.w1, SUB), (4, self.wr1, 15), (5, self.wd2, SUB), (6, self.wr2, SUB), (5, self.wd3, 4), (9, self.wr3, 4))[layer]
        base = 1 if layer == 1 else 0

        def emit(units, first, last):
            rows = side_by_side([join([lhs(unit, step) for unit in units]) for step in range(first, last)])
            acc = dot(rows, ref[first * WIDE:first * WIDE + rows.shape[1], :])
            for n, unit in enumerate(units):
                part = acc[n * UNIT:(n + 1) * UNIT]
                if layer == 0:
                    self.finish(layer, 2 * unit, part[:, :WIDE])
                    self.finish(layer, 2 * unit + 1, part[:, WIDE:])
                else:
                    self.finish(layer, unit, part)

        def chunk(c):
            emit([base + n for n in range(CHUNK * c, min(CHUNK * (c + 1), count))], 0, steps)

        items = [lambda c=c: chunk(c) for c in range(-(-count // CHUNK))]
        if layer == 1:
            items.append(lambda: (emit([0], 2, 4), emit([TILE], 0, 2)))

        def start():
            self.total = [jnp.zeros((TILE, WIDE), F32)] * 2

        def store():
            for n in range(2):
                self.sums[n] = self.total[n]

        return [start, *items, store]

    def finalize(self, layer):
        rep = (C1, C2, C3)[layer // 2]
        area = AREAS[layer // 2]
        per_strip = area * rep / (WIDE * SUB)
        count = float(area * rep // SUB)
        bias, gain, offset = self.vecs[layer, 0:1, :], self.vecs[layer, 1:2, :], self.vecs[layer, 2:3, :]
        plain, square = [self.sums[n, :SUB] + self.sums[n, SUB:] for n in range(2)]
        rest = join([plain + per_strip * bias, square + 2.0 * bias * plain + per_strip * bias * bias])
        parts = []
        for _ in range(3):
            parts.append(rest.astype(BF))
            rest = rest - parts[-1].astype(F32)
        grouped = dot(join(parts), self.gmat[layer // 2])
        grouped = grouped[:TILE] + grouped[TILE:2 * TILE] + grouped[2 * TILE:]
        mean = jnp.sum(grouped[:SUB], axis=0, keepdims=True) / count
        power = jnp.sum(grouped[SUB:], axis=0, keepdims=True) / count
        scale = lax.rsqrt(jnp.maximum(power - mean * mean, 0.0) + NORM_EPS) * gain
        self.affine = [jnp.broadcast_to(row, (TILE, WIDE)) for row in (scale, offset + (bias - mean) * scale)]

    def apply(self, block):
        return jnp.maximum(block * self.affine[0] + self.affine[1], 0.0)

    def row0(self, i):
        val = self.apply(self.abuf[i])
        self.y1e[i + 1, 0:SUB] = val[..., LOW].astype(BF)
        self.y1o[i + 1, 1:] = val[..., HIGH].astype(BF)
        self.y1o[i + 1, 0] = from_left(val[SUB - 1][:, HIGH], self.strip)
        self.y1e[i + 1, SUB] = from_right(val[0][:, LOW], self.strip)

    def row1(self, i):
        val = self.apply(self.abuf[i])
        if i in self.keep:
            val = val * self.keep[i]
        self.z1e[i] = val[..., LOW].astype(BF)
        self.z1o[i, 1:] = val[..., HIGH].astype(BF)
        self.z1o[i, 0] = from_left(val[SUB - 1][:, HIGH], self.strip)

    def row2(self, u):
        val = self.apply(self.abuf[u])
        for v, part in enumerate((LOW, HIGH)):
            line = val[..., part]
            self.y2[2 * u + v + 1, 1:SUB + 1] = line.astype(BF)
            self.y2[2 * u + v + 1, 0] = from_left(line[SUB - 1], self.strip)
            self.y2[2 * u + v + 1, SUB + 1] = from_right(line[0], self.strip)

    def row3(self, u):
        val = self.apply(self.abuf[u])
        for v, part in enumerate((LOW, HIGH)):
            for q in range(SUB):
                pixel = val[q][:, part]
                if q % 2:
                    self.z2o[2 * u + v + 1, q // 2 + 1] = pixel.astype(BF)
                else:
                    self.z2e[2 * u + v + 1, q // 2] = pixel.astype(BF)
            self.z2o[2 * u + v + 1, 0] = from_left(val[SUB - 1][:, part], self.strip)

    def row4(self, u):
        val = self.apply(self.abuf[u])
        for v in range(2):
            line = val[4 * v:4 * v + 4]
            self.y3[2 * u + v + 1, 1:5] = line.astype(BF)
            self.y3[2 * u + v + 1, 0] = side_by_side([from_left(line[3][:, part], self.strip) for part in (LOW, HIGH)])
            self.y3[2 * u + v + 1, 5] = side_by_side([from_right(line[0][:, part], self.strip) for part in (LOW, HIGH)])

    def row5(self, u):
        val = self.apply(self.abuf[u])
        for v in range(2):
            for h, part in enumerate((LOW, HIGH)):
                for q in range(4):
                    self.obuf[u, v, h, pl.ds(q, TILE, 4), :] = val[4 * v + q][:, part]
                for w in range(HALVES):
                    self.put(2 * u + w, v, part, self.obuf[u, v, h, 32 * w:32 * w + 32].astype(BF))

    def post(self, layer):
        row, count = ((self.row0, TILE), (self.row1, TILE + 1), (self.row2, SUB), (self.row3, SUB), (self.row4, 4), (self.row5, 4))[layer]
        return [lambda: self.finalize(layer)] + [lambda i=i: row(i) for i in range(count)]


def blend(chunks, rest):
    done = 0
    for n, emit in enumerate(chunks):
        emit()
        goal = len(rest) * (n + 1) // len(chunks)
        for item in rest[done:goal]:
            item()
        done = goal
    for item in rest[done:]:
        item()


def encoder_kernel(image, down1, v1, refine1, v2, down2, v3, refine2, v4, wd3, v5, wr3, v6, out, inbuf, outbuf, in_send, in_recv, out_send, out_recv, taps,
                   vecs, w1, wr1, wd2, wr2, perm, gmat, af, *buffers):
    group = pl.program_id(0)
    me = 2 * lax.axis_index("h") + lax.axis_index("w")

    def peer(k):
        return lax.rem(me + k, PEERS)

    def device(index):
        return {"h": index // 2, "w": lax.rem(index, 2)}

    def images(index, g):
        return pl.ds(index * PAIR * GROUPS + PAIR * g, PAIR)

    def send_in(g, to, sender):
        return pltpu.make_async_remote_copy(image.at[images(to, g)], inbuf.at[g, sender], in_send.at[g, to], in_recv.at[g, sender], device_id=device(to), device_id_type=MESH)

    def keep_in(g):
        return pltpu.make_async_copy(image.at[images(me, g)], inbuf.at[g, me], in_recv.at[g, me])

    def send_out(g, to, sender):
        return pltpu.make_async_remote_copy(outbuf.at[g, to], out.at[images(sender, g)], out_send.at[g, to], out_recv.at[g, sender], device_id=device(to), device_id_type=MESH)

    def keep_out(g):
        return pltpu.make_async_copy(outbuf.at[g, me], out.at[images(me, g)], out_recv.at[g, me])

    def start_out(g):
        for k in range(1, PEERS):
            send_out(g, peer(k), me).start()
        keep_out(g).start()

    @pl.when(group == 0)
    def _():
        barrier = pltpu.get_barrier_semaphore()
        for k in range(1, PEERS):
            pl.semaphore_signal(barrier, inc=1, device_id=device(peer(k)), device_id_type=MESH)
        pl.semaphore_wait(barrier, PEERS - 1)

        def begin(g, _):
            keep_in(g).start()
            for k in range(1, PEERS):
                send_in(g, peer(k), me).start()
            return 0

        lax.fori_loop(0, GROUPS, begin, 0)

        expand_first(down1, taps, w1)
        expand_refine1(refine1, wr1)
        expand_rows(down2, wd2, 2, lambda y, x: 6 * x + y)
        expand_rows(refine2, wr2, 1, lambda y, x: 3 * y + x)
        for i, ref in enumerate((v1, v2, v3, v4, v5, v6)):
            vecs[i] = side_by_side([ref[...]] * (WIDE // ref.shape[1]))
        row, lane = iota((2 * WIDE, LANES), 0), iota((2 * WIDE, LANES), 1)
        for d in range(PHASES):
            perm[:, d * LANES:(d + 1) * LANES] = one_hot(row == 4 * ((lane % TILE) * SUB + lane // TILE) + d - 1)
        row, lane = iota((WIDE, WIDE), 0), iota((WIDE, WIDE), 1)
        for g, rep in enumerate((C1, C2, C3)):
            gmat[g] = one_hot((row % rep) // (rep // SUB) == (lane % rep) // (rep // SUB))
        for e in range(PAIR):
            bs, _, y1e, y1o, _, _, y2, z2e, z2o, y3 = buffers[e:10 * PAIR:PAIR]
            for ref in (y1e, y1o, y2, y3, z2e, z2o, bs):
                ref[0] = jnp.zeros(ref.shape[1:], BF)
            for ref in (y1e, y1o, y2, y3):
                ref[ref.shape[0] - 1] = jnp.zeros(ref.shape[1:], BF)

    @pl.when(group > 0)
    def _():
        start_out(group - 1)

    keep_in(group).wait()
    for k in range(1, PEERS):
        send_in(group, peer(k), peer(k)).wait_recv()

    def put_of(e):
        def put(to, v, part, val):
            outbuf[group, to, e, v, :, part] = val

        return put

    params = (vecs, gmat, w1, wr1, wd2, wr2, wd3, wr3)
    streams = [Stream(params, buffers[e::PAIR], put_of(e)) for e in range(PAIR)]

    sides = [join([inbuf[group, HALVES * hh + half, e] for e in range(PAIR) for hh in range(4)]) for half in range(HALVES)]
    af[...] = dot(side_by_side(sides), perm[...]).reshape(af.shape)

    def im2col(e, k):
        rows = []
        for c in range(3):
            block = 24 * e + (k // 2) * 6 + c * 2 + k % 2
            rows += [af[block, :, d * LANES:(d + 1) * LANES] for d in range(PHASES)]
        rows.append(jnp.zeros((SUB, LANES), F32))
        streams[e].bs[k + 1] = join(rows).T.astype(BF).reshape(SUB, TILE, LANES)

    def phase(chunks, rest):
        pl.when(group >= 0)(lambda: blend(chunks, rest))

    gather = [[lambda e=e, k=k: im2col(e, k) for k in range(SUB)] for e in range(PAIR)]
    first, second = streams
    phase([], gather[0])
    phase(first.conv(0), gather[1])
    for layer in range(6):
        phase(second.conv(layer), first.post(layer))
        phase(first.conv(layer + 1) if layer < 5 else [], second.post(layer))

    @pl.when(group == GROUPS - 1)
    def _():
        def sent(g, _):
            for k in range(1, PEERS):
                send_in(g, peer(k), me).wait_send()
            return 0

        lax.fori_loop(0, GROUPS, sent, 0)
        start_out(group)

        def done(g, _):
            for k in range(1, PEERS):
                send_out(g, peer(k), me).wait_send()
                send_out(g, peer(k), peer(k)).wait_recv()
            keep_out(g).wait()
            return 0

        lax.fori_loop(0, GROUPS, done, 0)


def solution(mesh):
    act_spec = P("batch", "h", "w")
    sems = pltpu.SemaphoreType.DMA((GROUPS, PEERS))
    scratch = [
        ((GROUPS, PEERS, PAIR, PIECE_ROWS, PIECE_COLS), BF), ((GROUPS, PEERS, PAIR, 2, 32, WIDE), BF), None, None, None, None, ((32, C1), F32),
        ((6, 3, WIDE), F32), ((WIDE, 512), BF), ((1024, WIDE), BF), ((1152, WIDE), BF), ((1536, WIDE), BF),
        ((512, 640), BF), ((3, WIDE, WIDE), BF), ((48, SUB, 640), F32),
    ]
    for shape, dtype in (
        ((9, SUB, TILE, LANES), BF), ((17, SUB, TILE, WIDE), F32), ((18, 9, TILE, LANES), BF), ((18, 9, TILE, LANES), BF), ((17, 8, TILE, LANES), BF),
        ((17, 9, TILE, LANES), BF), ((18, 10, TILE, LANES), BF), ((17, 4, TILE, LANES), BF), ((17, 5, TILE, LANES), BF), ((10, 6, TILE, WIDE), BF),
        ((4, 2, 2, 64, LANES), F32), ((2, TILE, WIDE), F32), ((2, TILE, WIDE), F32),
    ):
        scratch += [(shape, dtype)] * PAIR

    def local_forward(tile, *params):
        planes = tile.transpose(0, 3, 1, 2).reshape(-1, PIECE_ROWS, PIECE_COLS)
        params = list(params)
        params[8], params[10] = params[8].reshape(-1, WIDE), params[10].reshape(-1, WIDE)
        return pl.pallas_call(
            encoder_kernel,
            grid=(GROUPS,),
            out_shape=jax.ShapeDtypeStruct((128, 2, 32, WIDE), BF),
            in_specs=[pl.BlockSpec(memory_space=pl.ANY)] + [pl.BlockSpec(memory_space=pltpu.VMEM)] * 12,
            out_specs=pl.BlockSpec(memory_space=pl.ANY),
            scratch_shapes=[sems if entry is None else pltpu.VMEM(*entry) for entry in scratch],
            compiler_params=pltpu.CompilerParams(vmem_limit_bytes=60 * 1024 * 1024, collective_id=0, has_side_effects=True),
            name="encoder",
        )(planes, *params)

    return jax.shard_map(local_forward, mesh=mesh, in_specs=(act_spec,) + (P(),) * 12, out_specs=act_spec, check_vma=False)
```

time: 530 us -> 143 us (0.27); the launches traced: 523 us -> 143 us
  blocking collectives: 249 us -> 0 us
  Pallas kernels: 0 us -> 138 us
  matrix products: 108 us -> 0 us
  other arithmetic: 55.3 us -> 0 us
  waiting for transfers between devices: 54.7 us -> 0 us
  starting transfers between devices: 37.3 us -> 0 us
  local copies, waits for them, and re-layouts: 17.2 us -> 5.04 us
    psum x6 -> x0, blocking collectives: 249 us -> none  [conv_norm(): totals = lax.psum(part_sums, ('h', 'w'))]
    pallas_call x0 -> x1, Pallas kernels: none -> 138 us  [local_forward(): pl.pallas_call(encoder_kernel, grid=(GROUPS,), out_shape=jax.ShapeDtypeSt...]
    conv_general_dilated x6 -> x0, matrix products: 108 us -> none  [conv_norm(): lax.conv_general_dilated(padded, kernel, (stride, stride), 'VALID', dimen...]
    ppermute x18 -> x0, waiting for transfers between devices: 54.7 us -> none  [shift_in(): return lax.ppermute(piece, axis_name, send_pairs)]
    convert_element_type x6 -> x0, other arithmetic: 53.5 us -> none  [norm_apply(): jax.nn.relu(summed * chan_scale[:, None, None, :] + chan_shift[:, None, N...]
    ppermute x18 -> x0, starting transfers between devices: 37.3 us -> none  [shift_in(): return lax.ppermute(piece, axis_name, send_pairs)]
  transfers between devices with their start and end apart: 18 -> 0, of which waited for: 18 -> 0; matrix products, arithmetic and copies ran while one was open for 0% -> 0% of each run, Pallas kernels for 0% -> 0%
where the time goes in v2:
time: 143 us
  Pallas kernels  138 us (97%)
  local copies, waits for them, and re-layouts  5.04 us (4%)
    pallas_call x1, Pallas kernels, local_forward(): pl.pallas_call(encoder_kernel, grid=(GROUPS,), out_shape=jax.ShapeDtypeSt...  138 us
    unnamed x1, local copies, waits for them, and re-layouts  5.04 us

profile of v2, /device:TPU:0, one launch (start us, length us, event | category | flops | bytes accessed | tf_op | source)
XLA Modules:
  0.0 142.8 jit_solution(1316719657058339057)
XLA Ops:
  0.0 137.8 %encoder.1 = bf16[128,2,32,256]{3,2,1,0:T(8,128)(2,1)} custom-call(bf16[128,48,256]{2,1,0:T(8,128)(2,1)} %bitcast.5, bf16[3,3,3,64]{3,2,1,0:T(4,128)(2,1)} %down1.1, f32[3,64]{1,0:T(4,128)} %v1.1, bf16[3,3,64,64]{3,2,1,0:T(8,128)(2,1)} %refine1.1, f32[3,64]{1,0:T(4,128)} %v2.1, bf16[3,3,64,128]{3,2,1,0:T(8,128)(2,1)} %down2.1, f32[3,128]{1,0:T(4,128)} %v3.1, ...), custom_call_target="tpu_custom_call" | custom-call | tf_op jit(solution)/shard_map/encoder/pallas_call | solution.py:412
  137.8 5.0 %copy.15 = bf16[128,2,32,256]{3,2,1,0:T(8,128)(2,1)} copy(bf16[128,2,32,256]{3,2,1,0:T(8,128)(2,1)} %encoder.1) | data formatting | bytes 8388608

commit v3 on v2

--- a/solution.py
+++ b/solution.py
@@ -9,7 +9,7 @@
 BF = jnp.bfloat16
 F32 = jnp.float32
 PAIR, SUB, TILE, LANES, WIDE, UNIT = 2, 8, 16, 128, 256, 128
-CHUNK = 4
+CHUNK = 2
 PEERS, GROUPS, HALVES = 8, 8, 2
 C1, C2, C3 = 64, 128, 256
 PHASES, PIECE_ROWS, PIECE_COLS = 5, 48, 256
@@ -96,7 +96,7 @@
 class Stream:
     def __init__(self, params, buffers, put):
         self.put = put
-        self.vecs, self.gmat, self.w1, self.wr1, self.wd2, self.wr2, self.wd3, self.wr3 = params
+        self.zero, self.vecs, self.gmat, self.w1, self.wr1, self.wd2, self.wr2, self.wd3, self.wr3 = params
         self.bs, self.abuf, self.y1e, self.y1o, self.z1e, self.z1o, self.y2, self.z2e, self.z2o, self.y3, self.obuf, self.sums, self.norm = buffers
         self.strip = iota((TILE, LANES), 0)
         upper = (iota((1, WIDE), 1) % LANES) < C1
@@ -149,28 +149,38 @@
         steps, ref, count = ((1, self.w1, SUB), (4, self.wr1, 15), (5, self.wd2, SUB), (6, self.wr2, SUB), (5, self.wd3, 4), (9, self.wr3, 4))[layer]
         base = 1 if layer == 1 else 0
 
+        waiting = []
+
+        def drain():
+            while waiting:
+                units, acc = waiting.pop(0)
+                for n, unit in enumerate(units):
+                    part = acc[n * UNIT:(n + 1) * UNIT]
+                    if layer == 0:
+                        self.finish(layer, 2 * unit, part[:, :WIDE])
+                        self.finish(layer, 2 * unit + 1, part[:, WIDE:])
+                    else:
+                        self.finish(layer, unit, part)
+
         def emit(units, first, last):
             rows = side_by_side([join([lhs(unit, step) for unit in units]) for step in range(first, last)])
             acc = dot(rows, ref[first * WIDE:first * WIDE + rows.shape[1], :])
-            for n, unit in enumerate(units):
-                part = acc[n * UNIT:(n + 1) * UNIT]
-                if layer == 0:
-                    self.finish(layer, 2 * unit, part[:, :WIDE])
-                    self.finish(layer, 2 * unit + 1, part[:, WIDE:])
-                else:
-                    self.finish(layer, unit, part)
+            drain()
+            waiting.append((units, acc))
 
         def chunk(c):
             emit([base + n for n in range(CHUNK * c, min(CHUNK * (c + 1), count))], 0, steps)
 
         items = [lambda c=c: chunk(c) for c in range(-(-count // CHUNK))]
         if layer == 1:
-            items.append(lambda: (emit([0], 2, 4), emit([TILE], 0, 2)))
+            items.append(lambda: emit([0], 2, 4))
+            items.append(lambda: emit([TILE], 0, 2))
 
         def start():
             self.total = [jnp.zeros((TILE, WIDE), F32)] * 2
 
         def store():
+            drain()
             for n in range(2):
                 self.sums[n] = self.total[n]
 
@@ -199,14 +209,14 @@
         return jnp.maximum(block * self.affine[0] + self.affine[1], 0.0)
 
     def row0(self, i):
-        val = self.apply(self.abuf[i])
+        val = self.apply(self.abuf[self.zero + i])
         self.y1e[i + 1, 0:SUB] = val[..., LOW].astype(BF)
         self.y1o[i + 1, 1:] = val[..., HIGH].astype(BF)
         self.y1o[i + 1, 0] = from_left(val[SUB - 1][:, HIGH], self.strip)
         self.y1e[i + 1, SUB] = from_right(val[0][:, LOW], self.strip)
 
     def row1(self, i):
-        val = self.apply(self.abuf[i])
+        val = self.apply(self.abuf[self.zero + i])
         if i in self.keep:
             val = val * self.keep[i]
         self.z1e[i] = val[..., LOW].astype(BF)
@@ -214,7 +224,7 @@
         self.z1o[i, 0] = from_left(val[SUB - 1][:, HIGH], self.strip)
 
     def row2(self, u):
-        val = self.apply(self.abuf[u])
+        val = self.apply(self.abuf[self.zero + u])
         for v, part in enumerate((LOW, HIGH)):
             line = val[..., part]
             self.y2[2 * u + v + 1, 1:SUB + 1] = line.astype(BF)
@@ -222,7 +232,7 @@
             self.y2[2 * u + v + 1, SUB + 1] = from_right(line[0], self.strip)
 
     def row3(self, u):
-        val = self.apply(self.abuf[u])
+        val = self.apply(self.abuf[self.zero + u])
         for v, part in enumerate((LOW, HIGH)):
             for q in range(SUB):
                 pixel = val[q][:, part]
@@ -233,7 +243,7 @@
             self.z2o[2 * u + v + 1, 0] = from_left(val[SUB - 1][:, part], self.strip)
 
     def row4(self, u):
-        val = self.apply(self.abuf[u])
+        val = self.apply(self.abuf[self.zero + u])
         for v in range(2):
             line = val[4 * v:4 * v + 4]
             self.y3[2 * u + v + 1, 1:5] = line.astype(BF)
@@ -241,7 +251,7 @@
             self.y3[2 * u + v + 1, 5] = side_by_side([from_right(line[0][:, part], self.strip) for part in (LOW, HIGH)])
 
     def row5(self, u):
-        val = self.apply(self.abuf[u])
+        val = self.apply(self.abuf[self.zero + u])
         for v in range(2):
             for h, part in enumerate((LOW, HIGH)):
                 for q in range(4):
@@ -345,7 +355,8 @@
 
         return put
 
-    params = (vecs, gmat, w1, wr1, wd2, wr2, wd3, wr3)
+    zero = (me + group) // (2 * TILE)
+    params = (zero, vecs, gmat, w1, wr1, wd2, wr2, wd3, wr3)
     streams = [Stream(params, buffers[e::PAIR], put_of(e)) for e in range(PAIR)]
 
     sides = [join([inbuf[group, HALVES * hh + half, e] for e in range(PAIR) for hh in range(4)]) for half in range(HALVES)]
@@ -359,16 +370,13 @@
         rows.append(jnp.zeros((SUB, LANES), F32))
         streams[e].bs[k + 1] = join(rows).T.astype(BF).reshape(SUB, TILE, LANES)
 
-    def phase(chunks, rest):
-        pl.when(group >= 0)(lambda: blend(chunks, rest))
-
     gather = [[lambda e=e, k=k: im2col(e, k) for k in range(SUB)] for e in range(PAIR)]
     first, second = streams
-    phase([], gather[0])
-    phase(first.conv(0), gather[1])
+    blend([], gather[0])
+    blend(first.conv(0), gather[1])
     for layer in range(6):
-        phase(second.conv(layer), first.post(layer))
-        phase(first.conv(layer + 1) if layer < 5 else [], second.post(layer))
+        blend(second.conv(layer), first.post(layer))
+        blend(first.conv(layer + 1) if layer < 5 else [], second.post(layer))
 
     @pl.when(group == GROUPS - 1)
     def _():

time: 143 us -> 117 us (0.82)
  Pallas kernels: 138 us -> 112 us
    pallas_call x1, Pallas kernels: 138 us -> 112 us  [local_forward(): pl.pallas_call(encoder_kernel, grid=(GROUPS,), out_shape=jax.ShapeDtypeSt...]
where the time goes in v3:
time: 117 us
  Pallas kernels  112 us (96%)
  local copies, waits for them, and re-layouts  5.04 us (4%)
    pallas_call x1, Pallas kernels, local_forward(): pl.pallas_call(encoder_kernel, grid=(GROUPS,), out_shape=jax.ShapeDtypeSt...  112 us
    unnamed x1, local copies, waits for them, and re-layouts  5.04 us

profile of v3, /device:TPU:0, one launch (start us, length us, event | category | flops | bytes accessed | tf_op | source)
XLA Modules:
  0.0 117.0 jit_solution(16083483358282496175)
XLA Ops:
  0.0 112.0 %encoder.1 = bf16[128,2,32,256]{3,2,1,0:T(8,128)(2,1)} custom-call(bf16[128,48,256]{2,1,0:T(8,128)(2,1)} %bitcast.5, bf16[3,3,3,64]{3,2,1,0:T(4,128)(2,1)} %down1.1, f32[3,64]{1,0:T(4,128)} %v1.1, bf16[3,3,64,64]{3,2,1,0:T(8,128)(2,1)} %refine1.1, f32[3,64]{1,0:T(4,128)} %v2.1, bf16[3,3,64,128]{3,2,1,0:T(8,128)(2,1)} %down2.1, f32[3,128]{1,0:T(4,128)} %v3.1, ...), custom_call_target="tpu_custom_call" | custom-call | tf_op jit(solution)/shard_map/encoder/pallas_call | solution.py:420
  112.0 5.0 %copy.15 = bf16[128,2,32,256]{3,2,1,0:T(8,128)(2,1)} copy(bf16[128,2,32,256]{3,2,1,0:T(8,128)(2,1)} %encoder.1) | data formatting | bytes 8388608

commit v4 on v3

--- a/solution.py
+++ b/solution.py
@@ -276,8 +276,8 @@
         item()
 
 
-def encoder_kernel(image, down1, v1, refine1, v2, down2, v3, refine2, v4, wd3, v5, wr3, v6, out, inbuf, outbuf, in_send, in_recv, out_send, out_recv, taps,
-                   vecs, w1, wr1, wd2, wr2, perm, gmat, af, *buffers):
+def encoder_kernel(image, down1, v1, refine1_in, v2, down2_in, v3, refine2_in, v4, wd3_in, v5, wr3_in, v6, out, inbuf, outbuf, in_send, in_recv, out_send, out_recv, taps,
+                   refine1, down2, refine2, wd3, wr3, load_sem, vecs, w1, wr1, wd2, wr2, perm, gmat, af, *buffers):
     group = pl.program_id(0)
     me = 2 * lax.axis_index("h") + lax.axis_index("w")
 
@@ -307,8 +307,41 @@
             send_out(g, peer(k), me).start()
         keep_out(g).start()
 
+    def wait_in(g):
+        keep_in(g).wait()
+        for k in range(1, PEERS):
+            send_in(g, peer(k), peer(k)).wait_recv()
+
+    def put_of(e):
+        def put(to, v, part, val):
+            outbuf[group, to, e, v, :, part] = val
+
+        return put
+
+    zero = (me + group) // (2 * TILE)
+    params = (zero, vecs, gmat, w1, wr1, wd2, wr2, wd3, wr3)
+    streams = [Stream(params, buffers[e::PAIR], put_of(e)) for e in range(PAIR)]
+
+    def permute(g):
+        sides = [join([inbuf[g, HALVES * hh + half, e] for e in range(PAIR) for hh in range(4)]) for half in range(HALVES)]
+        af[...] = dot(side_by_side(sides), perm[...]).reshape(af.shape)
+
+    def im2col(e, k):
+        rows = []
+        for c in range(3):
+            block = 24 * e + (k // 2) * 6 + c * 2 + k % 2
+            rows += [af[block, :, d * LANES:(d + 1) * LANES] for d in range(PHASES)]
+        rows.append(jnp.zeros((SUB, LANES), F32))
+        streams[e].bs[k + 1] = join(rows).T.astype(BF).reshape(SUB, TILE, LANES)
+
+    gather = [[lambda e=e, k=k: im2col(e, k) for k in range(SUB)] for e in range(PAIR)]
+
     @pl.when(group == 0)
     def _():
+        pairs = ((refine1_in, refine1), (down2_in, down2), (refine2_in, refine2), (wd3_in, wd3), (wr3_in, wr3))
+        loads = [pltpu.make_async_copy(*pair, load_sem.at[n]) for n, pair in enumerate(pairs)]
+        for load in loads:
+            load.start()
         barrier = pltpu.get_barrier_semaphore()
         for k in range(1, PEERS):
             pl.semaphore_signal(barrier, inc=1, device_id=device(peer(k)), device_id_type=MESH)
@@ -323,11 +356,13 @@
         lax.fori_loop(0, GROUPS, begin, 0)
 
         expand_first(down1, taps, w1)
+        for load in loads:
+            load.wait()
         expand_refine1(refine1, wr1)
         expand_rows(down2, wd2, 2, lambda y, x: 6 * x + y)
         expand_rows(refine2, wr2, 1, lambda y, x: 3 * y + x)
         for i, ref in enumerate((v1, v2, v3, v4, v5, v6)):
-            vecs[i] = side_by_side([ref[...]] * (WIDE // ref.shape[1]))
+            vecs[i, 0:3] = side_by_side([ref[...]] * (WIDE // ref.shape[1]))
         row, lane = iota((2 * WIDE, LANES), 0), iota((2 * WIDE, LANES), 1)
         for d in range(PHASES):
             perm[:, d * LANES:(d + 1) * LANES] = one_hot(row == 4 * ((lane % TILE) * SUB + lane // TILE) + d - 1)
@@ -338,45 +373,27 @@
             bs, _, y1e, y1o, _, _, y2, z2e, z2o, y3 = buffers[e:10 * PAIR:PAIR]
             for ref in (y1e, y1o, y2, y3, z2e, z2o, bs):
                 ref[0] = jnp.zeros(ref.shape[1:], BF)
-            for ref in (y1e, y1o, y2, y3):
-                ref[ref.shape[0] - 1] = jnp.zeros(ref.shape[1:], BF)
+            for ref, last in ((y1e, 17), (y1o, 17), (y2, 17), (y3, 9)):
+                ref[last] = jnp.zeros(ref.shape[1:], BF)
+
+        wait_in(0)
+        permute(0)
+        for item in (*gather[0], *gather[1], *streams[0].conv(0)):
+            item()
 
     @pl.when(group > 0)
     def _():
         start_out(group - 1)
 
-    keep_in(group).wait()
-    for k in range(1, PEERS):
-        send_in(group, peer(k), peer(k)).wait_recv()
-
-    def put_of(e):
-        def put(to, v, part, val):
-            outbuf[group, to, e, v, :, part] = val
-
-        return put
-
-    zero = (me + group) // (2 * TILE)
-    params = (zero, vecs, gmat, w1, wr1, wd2, wr2, wd3, wr3)
-    streams = [Stream(params, buffers[e::PAIR], put_of(e)) for e in range(PAIR)]
-
-    sides = [join([inbuf[group, HALVES * hh + half, e] for e in range(PAIR) for hh in range(4)]) for half in range(HALVES)]
-    af[...] = dot(side_by_side(sides), perm[...]).reshape(af.shape)
-
-    def im2col(e, k):
-        rows = []
-        for c in range(3):
-            block = 24 * e + (k // 2) * 6 + c * 2 + k % 2
-            rows += [af[block, :, d * LANES:(d + 1) * LANES] for d in range(PHASES)]
-        rows.append(jnp.zeros((SUB, LANES), F32))
-        streams[e].bs[k + 1] = join(rows).T.astype(BF).reshape(SUB, TILE, LANES)
-
-    gather = [[lambda e=e, k=k: im2col(e, k) for k in range(SUB)] for e in range(PAIR)]
     first, second = streams
-    blend([], gather[0])
-    blend(first.conv(0), gather[1])
+    following = lax.rem(group + 1, GROUPS)
     for layer in range(6):
-        blend(second.conv(layer), first.post(layer))
-        blend(first.conv(layer + 1) if layer < 5 else [], second.post(layer))
+        extra = gather[0] + gather[1] if layer == 5 else []
+        blend(second.conv(layer), first.post(layer) + extra)
+        if layer == 4:
+            pl.when(group < GROUPS - 1)(lambda: wait_in(following))
+        extra = [lambda: permute(following)] if layer == 4 else []
+        blend(extra + first.conv(layer + 1 if layer < 5 else 0), second.post(layer))
 
     @pl.when(group == GROUPS - 1)
     def _():
@@ -402,13 +419,14 @@
     act_spec = P("batch", "h", "w")
     sems = pltpu.SemaphoreType.DMA((GROUPS, PEERS))
     scratch = [
-        ((GROUPS, PEERS, PAIR, PIECE_ROWS, PIECE_COLS), BF), ((GROUPS, PEERS, PAIR, 2, 32, WIDE), BF), None, None, None, None, ((32, C1), F32),
-        ((6, 3, WIDE), F32), ((WIDE, 512), BF), ((1024, WIDE), BF), ((1152, WIDE), BF), ((1536, WIDE), BF),
+        ((GROUPS, PEERS, PAIR, PIECE_ROWS, PIECE_COLS), BF), ((GROUPS, PEERS, PAIR, 2, 32, WIDE), BF), sems, sems, sems, sems, ((32, C1), F32),
+        ((3, 3, C1, C1), BF), ((3, 3, C1, C2), BF), ((3, 3, C2, C2), BF), ((1152, WIDE), BF), ((2304, WIDE), BF), pltpu.SemaphoreType.DMA((5,)),
+        ((8, 8, WIDE), F32), ((WIDE, 512), BF), ((1024, WIDE), BF), ((1152, WIDE), BF), ((1536, WIDE), BF),
         ((512, 640), BF), ((3, WIDE, WIDE), BF), ((48, SUB, 640), F32),
     ]
     for shape, dtype in (
-        ((9, SUB, TILE, LANES), BF), ((17, SUB, TILE, WIDE), F32), ((18, 9, TILE, LANES), BF), ((18, 9, TILE, LANES), BF), ((17, 8, TILE, LANES), BF),
-        ((17, 9, TILE, LANES), BF), ((18, 10, TILE, LANES), BF), ((17, 4, TILE, LANES), BF), ((17, 5, TILE, LANES), BF), ((10, 6, TILE, WIDE), BF),
+        ((9, SUB, TILE, LANES), BF), ((17, SUB, TILE, WIDE), F32), ((20, 9, TILE, LANES), BF), ((20, 9, TILE, LANES), BF), ((17, 8, TILE, LANES), BF),
+        ((20, 9, TILE, LANES), BF), ((18, 10, TILE, LANES), BF), ((17, 4, TILE, LANES), BF), ((20, 5, TILE, LANES), BF), ((10, 6, TILE, WIDE), BF),
         ((4, 2, 2, 64, LANES), F32), ((2, TILE, WIDE), F32), ((2, TILE, WIDE), F32),
     ):
         scratch += [(shape, dtype)] * PAIR
@@ -417,15 +435,16 @@
         planes = tile.transpose(0, 3, 1, 2).reshape(-1, PIECE_ROWS, PIECE_COLS)
         params = list(params)
         params[8], params[10] = params[8].reshape(-1, WIDE), params[10].reshape(-1, WIDE)
-        return pl.pallas_call(
+        result = pl.pallas_call(
             encoder_kernel,
             grid=(GROUPS,),
             out_shape=jax.ShapeDtypeStruct((128, 2, 32, WIDE), BF),
-            in_specs=[pl.BlockSpec(memory_space=pl.ANY)] + [pl.BlockSpec(memory_space=pltpu.VMEM)] * 12,
+            in_specs=[pl.BlockSpec(memory_space=pltpu.HBM if n in (0, 3, 5, 7, 9, 11) else pltpu.VMEM) for n in range(13)],
             out_specs=pl.BlockSpec(memory_space=pl.ANY),
-            scratch_shapes=[sems if entry is None else pltpu.VMEM(*entry) for entry in scratch],
+            scratch_shapes=[pltpu.VMEM(*entry) if isinstance(entry, tuple) else entry for entry in scratch],
             compiler_params=pltpu.CompilerParams(vmem_limit_bytes=60 * 1024 * 1024, collective_id=0, has_side_effects=True),
             name="encoder",
         )(planes, *params)
+        return jnp.maximum(result, 0)
 
     return jax.shard_map(local_forward, mesh=mesh, in_specs=(act_spec,) + (P(),) * 12, out_specs=act_spec, check_vma=False)

time: 117 us -> 110 us (0.940)
  Pallas kernels: 112 us -> 105 us
  local copies, waits for them, and re-layouts: 5.04 us -> 0 us
  other arithmetic: 0 us -> 4.47 us
    pallas_call x1, Pallas kernels: 112 us -> 105 us  [local_forward(): pl.pallas_call(encoder_kernel, grid=(GROUPS,), out_shape=jax.ShapeDtypeSt...]
    unnamed x1 -> x0, local copies, waits for them, and re-layouts: 5.04 us -> none
    max x0 -> x1, other arithmetic: none -> 4.47 us  [local_forward(): return jnp.maximum(result, 0)]
where the time goes in v4:
time: 110 us; the launch traced here: 109 us
  Pallas kernels  105 us (95%)
  other arithmetic  4.47 us (4%)
    pallas_call x1, Pallas kernels, local_forward(): pl.pallas_call(encoder_kernel, grid=(GROUPS,), out_shape=jax.ShapeDtypeSt...  105 us
    max x1, other arithmetic, local_forward(): return jnp.maximum(result, 0)  4.47 us

profile of v4, /device:TPU:0, one launch (start us, length us, event | category | flops | bytes accessed | tf_op | source)
XLA Modules:
  0.0 109.5 jit_solution(278578445860979795)
XLA Ops:
  0.0 105.0 %encoder.1 = bf16[128,2,32,256]{3,2,1,0:T(8,128)(2,1)} custom-call(bf16[128,48,256]{2,1,0:T(8,128)(2,1)} %bitcast.5, bf16[3,3,3,64]{3,2,1,0:T(4,128)(2,1)} %down1.1, f32[3,64]{1,0:T(4,128)} %v1.1, bf16[3,3,64,64]{3,2,1,0:T(8,128)(2,1)} %refine1_in.1, f32[3,64]{1,0:T(4,128)} %v2.1, bf16[3,3,64,128]{3,2,1,0:T(8,128)(2,1)} %down2_in.1, f32[3,128]{1,0:T(4,128)} %v3.1, ...), custom_call_target="tpu_custom_call" | custom-call | tf_op jit(solution)/shard_map/encoder/pallas_call | solution.py:438
  105.0 4.5 %broadcast_maximum_fusion = bf16[128,2,32,256]{3,2,1,0:T(8,128)(2,1)} fusion(bf16[128,2,32,256]{3,2,1,0:T(8,128)(2,1)} %encoder.1), kind=kLoop, calls=%fused_computation | loop fusion | flops 2097152 | bytes 8388608 | tf_op jit(solution)/shard_map/max | solution.py:448

commit v5 on v4

--- a/solution.py
+++ b/solution.py
@@ -97,8 +97,9 @@
     def __init__(self, params, buffers, put):
         self.put = put
         self.zero, self.vecs, self.gmat, self.w1, self.wr1, self.wd2, self.wr2, self.wd3, self.wr3 = params
-        self.bs, self.abuf, self.y1e, self.y1o, self.z1e, self.z1o, self.y2, self.z2e, self.z2o, self.y3, self.obuf, self.sums, self.norm = buffers
+        self.bs, self.abuf, self.y1e, self.y1o, self.z1e, self.z1o, self.y2, self.z2e, self.z2o, self.y3, self.obuf, self.sums, self.z1m = buffers
         self.strip = iota((TILE, LANES), 0)
+        self.lane = iota((TILE, LANES), 1)
         upper = (iota((1, WIDE), 1) % LANES) < C1
         self.keep = {0: jnp.where(upper, 0.0, 1.0), TILE: jnp.where(upper, 1.0, 0.0)}
 
@@ -113,13 +114,10 @@
         return side_by_side([tile(2 * step), tile(2 * step + 1)]) if step < 4 else tile(2 * step)
 
     def lhs2(self, unit, step):
-        taps = ((self.z1o, 0), (self.z1e, 0), (self.z1o, 1))
-
-        def tile(n):
-            ref, first = taps[n // 3]
-            return rows_of(ref, 2 * unit + n % 3, first, SUB)
-
-        return self.ninth(tile, step)
+        if step < 3:
+            ref, first = ((self.z1o, 0), (self.z1e, 0), (self.z1o, 1))[step]
+            return side_by_side([rows_of(ref, 2 * unit + n, first, SUB) for n in range(2)])
+        return side_by_side([rows_of(self.z1m, unit, 0, SUB), rows_of(self.z1o, 2 * unit + 2, 1, SUB)])
 
     def lhs3(self, unit, step):
         return side_by_side([rows_of(self.y2, 2 * unit + n // 3, n % 3, SUB) for n in (2 * step, 2 * step + 1)])
@@ -146,7 +144,7 @@
 
     def conv(self, layer):
         lhs = (self.lhs0, self.lhs1, self.lhs2, self.lhs3, self.lhs4, self.lhs5)[layer]
-        steps, ref, count = ((1, self.w1, SUB), (4, self.wr1, 15), (5, self.wd2, SUB), (6, self.wr2, SUB), (5, self.wd3, 4), (9, self.wr3, 4))[layer]
+        steps, ref, count = ((1, self.w1, SUB), (4, self.wr1, 15), (4, self.wd2, SUB), (6, self.wr2, SUB), (5, self.wd3, 4), (9, self.wr3, 4))[layer]
         base = 1 if layer == 1 else 0
 
         waiting = []
@@ -221,7 +219,13 @@
             val = val * self.keep[i]
         self.z1e[i] = val[..., LOW].astype(BF)
         self.z1o[i, 1:] = val[..., HIGH].astype(BF)
-        self.z1o[i, 0] = from_left(val[SUB - 1][:, HIGH], self.strip)
+        edge = from_left(val[SUB - 1][:, HIGH], self.strip)
+        self.z1o[i, 0] = edge
+        if i and i % 2 == 0:
+            for q in range(SUB):
+                left = val[q - 1][:, HIGH] if q else edge.astype(F32)
+                shifted = pltpu.roll(val[q][:, LOW], C1, 1)
+                self.z1m[i // 2 - 1, q] = jnp.where(self.lane < C1, left, shifted).astype(BF)
 
     def row2(self, u):
         val = self.apply(self.abuf[self.zero + u])
@@ -359,7 +363,7 @@
         for load in loads:
             load.wait()
         expand_refine1(refine1, wr1)
-        expand_rows(down2, wd2, 2, lambda y, x: 6 * x + y)
+        expand_rows(down2, wd2, 2, lambda y, x: 4 * x + y if y < 4 else 12 + x)
         expand_rows(refine2, wr2, 1, lambda y, x: 3 * y + x)
         for i, ref in enumerate((v1, v2, v3, v4, v5, v6)):
             vecs[i, 0:3] = side_by_side([ref[...]] * (WIDE // ref.shape[1]))
@@ -421,13 +425,13 @@
     scratch = [
         ((GROUPS, PEERS, PAIR, PIECE_ROWS, PIECE_COLS), BF), ((GROUPS, PEERS, PAIR, 2, 32, WIDE), BF), sems, sems, sems, sems, ((32, C1), F32),
         ((3, 3, C1, C1), BF), ((3, 3, C1, C2), BF), ((3, 3, C2, C2), BF), ((1152, WIDE), BF), ((2304, WIDE), BF), pltpu.SemaphoreType.DMA((5,)),
-        ((8, 8, WIDE), F32), ((WIDE, 512), BF), ((1024, WIDE), BF), ((1152, WIDE), BF), ((1536, WIDE), BF),
+        ((8, 8, WIDE), F32), ((WIDE, 512), BF), ((1024, WIDE), BF), ((1024, WIDE), BF), ((1536, WIDE), BF),
         ((512, 640), BF), ((3, WIDE, WIDE), BF), ((48, SUB, 640), F32),
     ]
     for shape, dtype in (
         ((9, SUB, TILE, LANES), BF), ((17, SUB, TILE, WIDE), F32), ((20, 9, TILE, LANES), BF), ((20, 9, TILE, LANES), BF), ((17, 8, TILE, LANES), BF),
         ((20, 9, TILE, LANES), BF), ((18, 10, TILE, LANES), BF), ((17, 4, TILE, LANES), BF), ((20, 5, TILE, LANES), BF), ((10, 6, TILE, WIDE), BF),
-        ((4, 2, 2, 64, LANES), F32), ((2, TILE, WIDE), F32), ((2, TILE, WIDE), F32),
+        ((4, 2, 2, 64, LANES), F32), ((2, TILE, WIDE), F32), ((8, SUB, TILE, LANES), BF),
     ):
         scratch += [(shape, dtype)] * PAIR
 

time: 110 us -> 107 us (0.973)
  Pallas kernels: 105 us -> 103 us
    pallas_call x1, Pallas kernels: 105 us -> 103 us  [local_forward(): pl.pallas_call(encoder_kernel, grid=(GROUPS,), out_shape=jax.ShapeDtypeSt...]
where the time goes in v5:
time: 107 us
  Pallas kernels  103 us (96%)
  other arithmetic  4.47 us (4%)
    pallas_call x1, Pallas kernels, local_forward(): pl.pallas_call(encoder_kernel, grid=(GROUPS,), out_shape=jax.ShapeDtypeSt...  103 us
    max x1, other arithmetic, local_forward(): return jnp.maximum(result, 0)  4.47 us

profile of v5, /device:TPU:0, one launch (start us, length us, event | category | flops | bytes accessed | tf_op | source)
XLA Modules:
  0.0 107.0 jit_solution(16649020863413547221)
XLA Ops:
  0.0 102.5 %encoder.1 = bf16[128,2,32,256]{3,2,1,0:T(8,128)(2,1)} custom-call(bf16[128,48,256]{2,1,0:T(8,128)(2,1)} %bitcast.5, bf16[3,3,3,64]{3,2,1,0:T(4,128)(2,1)} %down1.1, f32[3,64]{1,0:T(4,128)} %v1.1, bf16[3,3,64,64]{3,2,1,0:T(8,128)(2,1)} %refine1_in.1, f32[3,64]{1,0:T(4,128)} %v2.1, bf16[3,3,64,128]{3,2,1,0:T(8,128)(2,1)} %down2_in.1, f32[3,128]{1,0:T(4,128)} %v3.1, ...), custom_call_target="tpu_custom_call" | custom-call | tf_op jit(solution)/shard_map/encoder/pallas_call | solution.py:442
  102.5 4.5 %broadcast_maximum_fusion = bf16[128,2,32,256]{3,2,1,0:T(8,128)(2,1)} fusion(bf16[128,2,32,256]{3,2,1,0:T(8,128)(2,1)} %encoder.1), kind=kLoop, calls=%fused_computation | loop fusion | flops 2097152 | bytes 8388608 | tf_op jit(solution)/shard_map/max | solution.py:452

commit v6 on v5

--- a/solution.py
+++ b/solution.py
@@ -295,26 +295,27 @@
         return pl.ds(index * PAIR * GROUPS + PAIR * g, PAIR)
 
     def send_in(g, to, sender):
-        return pltpu.make_async_remote_copy(image.at[images(to, g)], inbuf.at[g, sender], in_send.at[g, to], in_recv.at[g, sender], device_id=device(to), device_id_type=MESH)
+        return pltpu.make_async_remote_copy(image.at[images(to, g)], inbuf.at[g, sender], in_send, in_recv.at[g], device_id=device(to), device_id_type=MESH)
 
     def keep_in(g):
-        return pltpu.make_async_copy(image.at[images(me, g)], inbuf.at[g, me], in_recv.at[g, me])
+        return pltpu.make_async_copy(image.at[images(me, g)], inbuf.at[g, me], in_recv.at[g])
 
     def send_out(g, to, sender):
-        return pltpu.make_async_remote_copy(outbuf.at[g, to], out.at[images(sender, g)], out_send.at[g, to], out_recv.at[g, sender], device_id=device(to), device_id_type=MESH)
+        return pltpu.make_async_remote_copy(outbuf.at[g, to], out.at[images(sender, g)], out_send, out_recv, device_id=device(to), device_id_type=MESH)
 
     def keep_out(g):
-        return pltpu.make_async_copy(outbuf.at[g, me], out.at[images(me, g)], out_recv.at[g, me])
+        return pltpu.make_async_copy(outbuf.at[g, me], out.at[images(me, g)], out_recv)
 
     def start_out(g):
         for k in range(1, PEERS):
             send_out(g, peer(k), me).start()
         keep_out(g).start()
 
+    def wait_for(ref, sem):
+        pltpu.make_async_copy(ref, ref, sem).wait()
+
     def wait_in(g):
-        keep_in(g).wait()
-        for k in range(1, PEERS):
-            send_in(g, peer(k), peer(k)).wait_recv()
+        wait_for(inbuf.at[g], in_recv.at[g])
 
     def put_of(e):
         def put(to, v, part, val):
@@ -401,29 +402,18 @@
 
     @pl.when(group == GROUPS - 1)
     def _():
-        def sent(g, _):
-            for k in range(1, PEERS):
-                send_in(g, peer(k), me).wait_send()
-            return 0
-
-        lax.fori_loop(0, GROUPS, sent, 0)
+        others = pl.ds(0, PAIR * GROUPS * (PEERS - 1))
+        wait_for(image.at[others], in_send)
         start_out(group)
-
-        def done(g, _):
-            for k in range(1, PEERS):
-                send_out(g, peer(k), me).wait_send()
-                send_out(g, peer(k), peer(k)).wait_recv()
-            keep_out(g).wait()
-            return 0
-
-        lax.fori_loop(0, GROUPS, done, 0)
+        wait_for(out.at[others], out_send)
+        wait_for(out, out_recv)
 
 
 def solution(mesh):
     act_spec = P("batch", "h", "w")
-    sems = pltpu.SemaphoreType.DMA((GROUPS, PEERS))
+    sem = pltpu.SemaphoreType.DMA
     scratch = [
-        ((GROUPS, PEERS, PAIR, PIECE_ROWS, PIECE_COLS), BF), ((GROUPS, PEERS, PAIR, 2, 32, WIDE), BF), sems, sems, sems, sems, ((32, C1), F32),
+        ((GROUPS, PEERS, PAIR, PIECE_ROWS, PIECE_COLS), BF), ((GROUPS, PEERS, PAIR, 2, 32, WIDE), BF), sem, sem((GROUPS,)), sem, sem, ((32, C1), F32),
         ((3, 3, C1, C1), BF), ((3, 3, C1, C2), BF), ((3, 3, C2, C2), BF), ((1152, WIDE), BF), ((2304, WIDE), BF), pltpu.SemaphoreType.DMA((5,)),
         ((8, 8, WIDE), F32), ((WIDE, 512), BF), ((1024, WIDE), BF), ((1024, WIDE), BF), ((1536, WIDE), BF),
         ((512, 640), BF), ((3, WIDE, WIDE), BF), ((48, SUB, 640), F32),

time: 107 us -> 105 us (0.981)
  Pallas kernels: 103 us -> 100 us
    pallas_call x1, Pallas kernels: 103 us -> 100 us  [local_forward(): pl.pallas_call(encoder_kernel, grid=(GROUPS,), out_shape=jax.ShapeDtypeSt...]
where the time goes in v6:
time: 105 us; the launch traced here: 104 us
  Pallas kernels  100 us (95%)
  other arithmetic  4.47 us (4%)
    pallas_call x1, Pallas kernels, local_forward(): pl.pallas_call(encoder_kernel, grid=(GROUPS,), out_shape=jax.ShapeDtypeSt...  100 us
    max x1, other arithmetic, local_forward(): return jnp.maximum(result, 0)  4.47 us

profile of v6, /device:TPU:0, one launch (start us, length us, event | category | flops | bytes accessed | tf_op | source)
XLA Modules:
  0.0 104.4 jit_solution(5838386611221531248)
XLA Ops:
  0.0 100.0 %encoder.1 = bf16[128,2,32,256]{3,2,1,0:T(8,128)(2,1)} custom-call(bf16[128,48,256]{2,1,0:T(8,128)(2,1)} %bitcast.5, bf16[3,3,3,64]{3,2,1,0:T(4,128)(2,1)} %down1.1, f32[3,64]{1,0:T(4,128)} %v1.1, bf16[3,3,64,64]{3,2,1,0:T(8,128)(2,1)} %refine1_in.1, f32[3,64]{1,0:T(4,128)} %v2.1, bf16[3,3,64,128]{3,2,1,0:T(8,128)(2,1)} %down2_in.1, f32[3,128]{1,0:T(4,128)} %v3.1, ...), custom_call_target="tpu_custom_call" | custom-call | tf_op jit(solution)/shard_map/encoder/pallas_call | solution.py:432
  100.0 4.5 %broadcast_maximum_fusion = bf16[128,2,32,256]{3,2,1,0:T(8,128)(2,1)} fusion(bf16[128,2,32,256]{3,2,1,0:T(8,128)(2,1)} %encoder.1), kind=kLoop, calls=%fused_computation | loop fusion | flops 2097152 | bytes 8388608 | tf_op jit(solution)/shard_map/max | solution.py:442
